TPU v7x, 256 devices: a whole 4x4x8 slice. The times are simulated.
256 devices in a mesh: site: 64 (over z, x, core), dom: 4 (over y).
Axes of the slice: x: 4, y: 4, z: 8, core: 2. Of those that a mesh axis runs over, the one named last changes fastest.
Arguments:
- top_partial: float32 [16, 61, 4, 65536], P(None, None, 'dom', 'site'), may hold values from 0.001 to 1
- bottom_partial: float32 [16, 61, 4, 65536], P(None, None, 'dom', 'site'), may hold values from 0.001 to 1
- left_vectors: float32 [256, 61, 61], P('dom'), may hold values from 0.05 to 1
- right_vectors: float32 [256, 61, 61], P('dom'), may hold values from 0.05 to 1
- decay_rates: float32 [256, 61], P('dom'), may hold values from 0.05 to 8
- state_weights: float32 [256, 61], P('dom'), may hold values from 0.002 to 0.05
- part_rates: float32 [256], P('dom'), may hold values from 0.3 to 3
- branch_lengths: float32 [1997], replicated, may hold values from 0.02 to 0.5
- pattern_weights: int32 [4, 65536], P('dom', 'site'), may hold values from 0 to 9
- block_partition: int32 [4, 512], P('dom', 'site'), may hold values from 0 to 255
- chosen_branches: int32 [16], replicated, may hold values from 0 to 1996, as said below
Outputs:
- site_loglik: float32 [16, 4, 65536], P(None, 'dom', 'site')
- part_derivs: float32 [2, 16, 256], P(None, None, 'dom')
- new_lengths: float32 [1997], replicated
Inputs may be any that keep to these rules, and one draw needn't show every extreme that they name: `chosen_branches`: distinct branch numbers.
All inputs are finite; a program needn't handle non-finite values.
Results may differ from a plain program's by a relative error of at most 0.0003.
Values sent between devices are 32-bit elements; how exact they have to be, the bound alone decides.
A program may use at most 64 MiB of HBM per device.

v0:
```python
import math

import jax
import jax.numpy as jnp
from jax import lax
from jax.sharding import PartitionSpec as P

BLK = 128


def in_one_piece(arrays, axis, split_dim, concat_dim, along):
    widths = [math.prod(a.shape[along:]) for a in arrays]
    both = jnp.concatenate(
        [a.reshape(*a.shape[:along], w) for a, w in zip(arrays, widths)], axis=along
    )
    out = lax.all_to_all(both, axis, split_axis=split_dim, concat_axis=concat_dim, tiled=True)
    parts = jnp.split(out, [sum(widths[:k]) for k in range(1, len(widths))], axis=along)
    return tuple((b.reshape(*out.shape[:along], *a.shape[along:]) for a, b in zip(arrays, parts)))


def cut_along(x, dim, count):
    dims = x.shape
    parts = x.reshape(*dims[:dim], count, dims[dim] // count, *dims[dim + 1 :])
    return jnp.moveaxis(parts, dim, 0)


def sum_at_owner(x, axis, dim):
    count = lax.axis_size(axis)
    parts = lax.all_to_all(cut_along(x, dim, count), axis, 0, 0, tiled=True)
    return jnp.sum(parts, axis=0)


def copy_for_each(x, axis):
    count = lax.axis_size(axis)
    return lax.all_to_all(jnp.broadcast_to(x[None], (count, *x.shape)), axis, 0, 0, tiled=True)


def of_everyone(x, axis):
    return copy_for_each(x, axis).sum(axis=0)


def project(upper, lower, vec_left, vec_right, state_w):
    scaled = upper * jnp.transpose(state_w)[None, :, :, None]
    lefts = jnp.einsum("binl,nik->bknl", scaled, vec_left, precision=lax.Precision.HIGHEST)
    rights = jnp.einsum("nkj,bjnl->bknl", vec_right, lower, precision=lax.Precision.HIGHEST)
    return (lefts, rights)


def finish(lefts, rights, exponent, times, weight_f):
    joint = lefts * rights
    expo = jnp.transpose(exponent)[None, :, :, None]
    decayed = joint * jnp.exp(expo * times[:, None, None, None])
    like_zero = jnp.sum(decayed, axis=1)
    like_one = jnp.sum(decayed * expo, axis=1)
    like_two = jnp.sum(decayed * expo * expo, axis=1)
    first = like_one / like_zero
    second = like_two / like_zero - first * first
    loglik = weight_f[None] * jnp.log(like_zero)
    sums = jnp.stack(
        [jnp.sum(weight_f[None] * first, axis=-1), jnp.sum(weight_f[None] * second, axis=-1)]
    )
    return (loglik, sums)


def on_device(
    top_partial,
    bottom_partial,
    left_vectors,
    right_vectors,
    decay_rates,
    state_weights,
    part_rates,
    branch_lengths,
    pattern_weights,
    block_partition,
    chosen_branches,
):
    times = branch_lengths[chosen_branches]
    branches = top_partial.shape[0]
    states = top_partial.shape[1]
    sites_here = top_partial.shape[3]
    nblocks = sites_here // BLK
    upper = top_partial.reshape(branches, states, nblocks, BLK)
    lower = bottom_partial.reshape(branches, states, nblocks, BLK)
    blocks = block_partition[0]
    owned = left_vectors.shape[0]
    groups = lax.axis_size("dom")
    parts_all = owned * groups
    wanted = lax.all_gather(block_partition, "dom", axis=0, tiled=True)
    relative = wanted - lax.axis_index("dom") * owned
    inside = jnp.logical_and(relative >= 0, relative < owned).astype(jnp.float32)
    clipped = jnp.clip(relative, 0, owned - 1)
    send_left = left_vectors[clipped] * inside[:, :, None, None]
    send_right = right_vectors[clipped] * inside[:, :, None, None]
    send_decay = decay_rates[clipped] * inside[:, :, None]
    send_weight = state_weights[clipped] * inside[:, :, None]
    send_rate = part_rates[clipped] * inside
    received = in_one_piece(
        (send_left, send_right, send_decay, send_weight, send_rate), "dom", 0, 0, 2
    )
    vec_left = jnp.sum(received[0], axis=0)
    vec_right = jnp.sum(received[1], axis=0)
    decay_b = jnp.sum(received[2], axis=0)
    weight_b = jnp.sum(received[3], axis=0)
    rate_b = jnp.sum(received[4], axis=0)
    exponent = -decay_b * rate_b[:, None]
    lefts, rights = project(upper, lower, vec_left, vec_right, weight_b)
    weight_f = pattern_weights[0].astype(jnp.float32).reshape(nblocks, BLK)
    loglik, sums = finish(lefts, rights, exponent, times, weight_f)
    onehot = (blocks[:, None] == jnp.arange(parts_all, dtype=jnp.int32)[None, :]).astype(
        jnp.float32
    )
    part_local = jnp.einsum("abn,np->abp", sums, onehot, precision=lax.Precision.HIGHEST)
    share = sum_at_owner(part_local, "dom", 2)
    share = of_everyone(share, "site")
    totals = of_everyone(jnp.sum(share, axis=2), "dom")
    updated = times - totals[0] / totals[1]
    new_lengths = branch_lengths.at[chosen_branches].set(updated)
    return (loglik.reshape(branches, 1, sites_here), share, new_lengths)


def solution(mesh):
    return jax.shard_map(
        on_device,
        mesh=mesh,
        in_specs=(
            P(None, None, "dom", "site"),
            P(None, None, "dom", "site"),
            P("dom", None, None),
            P("dom", None, None),
            P("dom", None),
            P("dom", None),
            P("dom"),
            P(),
            P("dom", "site"),
            P("dom", "site"),
            P(),
        ),
        out_specs=(P(None, "dom", "site"), P(None, None, "dom"), P()),
        check_vma=False,
    )
```

profile of v0, /device:TPU:1, one launch (start us, length us, event | category | flops | bytes accessed | tf_op | source)
XLA Modules:
  0.0 120.6 jit_solution(9104302624612339698)
XLA Ops:
  0.6 0.0 copy-start
  0.6 0.8 copy.97
  1.5 8.9 %all-gather = s32[4,1,8]{2,1,0:T(1,128)S(1)} all-gather(s32[1,1,8]{2,1,0:T(1,128)} %bitcast.49), channel_id=1, replica_groups=mesh['site'=64,'dom'=4] {'dom'}, dimensions={0}, use_global_device_ids=true | all-gather | bytes 160 | tf_op jit(solution)/shard_map/all_gather | solution.py:89
  10.5 0.1 reshape.90
  10.5 1.4 %gather_fusion.4 = f32[32]{0:T(128)S(1)} fusion(f32[64]{0:T(128)} %param.17, s32[1024]{0:T(1024)S(1)} %pad_clamp_fusion.1), kind=kCustom, calls=%fused_computation.4 | custom fusion | bytes 384 | tf_op jit(solution)/shard_map/gather | solution.py:97
  11.9 0.1 reshape.121
  12.0 0.6 select_bitcast_fusion
  12.6 0.0 copy-done
  12.6 2.7 %gather_fusion = f32[32,61,61]{2,0,1:T(8,128)S(1)} fusion(f32[64,61,61]{2,0,1:T(8,128)S(1)} %copy-done, s32[1024]{0:T(1024)S(1)} %pad_clamp_fusion.1), kind=kCustom, calls=%fused_computation | custom fusion | bytes 952704 | tf_op jit(solution)/shard_map/gather | solution.py:93
  15.3 1.6 %copy.60 = f32[32,61,61]{2,1,0:T(8,128)} copy(f32[32,61,61]{2,0,1:T(8,128)S(1)} %gather_fusion) | data formatting | bytes 952576 | tf_op jit(solution)/shard_map/gather | solution.py:93
  16.9 1.7 %gather.23 = f32[4,8,3721]{2,1,0:T(8,128)S(1)} reshape(f32[32,61,61]{2,1,0:T(8,128)} %copy.60) | data formatting | bytes 952576 | tf_op jit(solution)/shard_map/gather | solution.py:93
  18.6 0.0 copy-start.2
  18.6 3.7 %gather_fusion.1 = f32[32,61,61]{2,0,1:T(8,128)S(1)} fusion(f32[64,61,61]{2,0,1:T(8,128)} %param.14, s32[1024]{0:T(1024)S(1)} %pad_clamp_fusion.1), kind=kCustom, calls=%fused_computation.1 | custom fusion | bytes 952704 | tf_op jit(solution)/shard_map/gather | solution.py:94
  22.3 1.6 %copy.61 = f32[32,61,61]{2,1,0:T(8,128)} copy(f32[32,61,61]{2,0,1:T(8,128)S(1)} %gather_fusion.1) | data formatting | bytes 952576 | tf_op jit(solution)/shard_map/gather | solution.py:94
  23.9 1.7 %gather.25 = f32[4,8,3721]{2,1,0:T(8,128)S(1)} reshape(f32[32,61,61]{2,1,0:T(8,128)} %copy.61) | data formatting | bytes 952576 | tf_op jit(solution)/shard_map/gather | solution.py:94
  25.6 0.0 copy-done.2
  25.6 0.6 gather_fusion.2
  26.2 1.3 %gather_fusion.3 = f32[32,61]{1,0:T(8,128)S(1)} fusion(f32[64,61]{1,0:T(8,128)} %param.16, s32[1024]{0:T(1024)S(1)} %pad_clamp_fusion.1), kind=kCustom, calls=%fused_computation.3 | custom fusion | bytes 15744 | tf_op jit(solution)/shard_map/gather | solution.py:96
  27.6 0.8 copy.62
  28.3 0.9 broadcast_multiply_fusion
  29.2 0.1 bitcast_multiply_fusion.1
  29.3 2.2 %concatenate.3 = f32[4,8,7565]{2,1,0:T(8,128)} concatenate(f32[4,8,3721]{2,1,0:T(8,128)} %get-tuple-element.29, f32[4,8,3721]{2,1,0:T(8,128)S(1)} %get-tuple-element.28, f32[4,8,61]{2,1,0:T(8,128)S(1)} %get-tuple-element.27, f32[4,8,61]{2,1,0:T(8,128)S(1)} %get-tuple-element.26, f32[4,8,1]{2,1,0:T(8,128)S(1)} %copy.62), dimensions={2} | concatenate | bytes 1936640 | tf_op jit(solution)/shard_map/concatenate | solution.py:13
  31.5 3.5 %all-to-all-start = ((f32[4,8,7565]{2,1,0:T(8,128)}), f32[4,8,7565]{2,1,0:T(8,128)S(1)}, u32[]{:S(2)}, u32[]{:S(2)}) async-start(f32[4,8,7565]{2,1,0:T(8,128)} %concatenate.3), calls=%async_computation | async-start | bytes 1966080 | tf_op jit(solution)/shard_map/all_to_all | solution.py:16
  35.1 0.7 convert_element_type.18
  35.7 0.7 compare_select_fusion.1
  36.4 0.7 gather_fusion.5
  37.1 9.3 %all-to-all-done = f32[4,8,7565]{2,1,0:T(8,128)S(1)} async-done(((f32[4,8,7565]{2,1,0:T(8,128)}), f32[4,8,7565]{2,1,0:T(8,128)S(1)}, u32[]{:S(2)}, u32[]{:S(2)}) %all-to-all-start) | async-done | bytes 968352 | tf_op jit(solution)/shard_map/all_to_all | solution.py:16
  46.3 0.2 slice_reduce_fusion.1
  46.5 0.3 reshape.171
  46.8 1.0 reduce_sum.131
  47.8 0.1 slice_reduce_fusion.4
  47.9 0.2 slice_reduce_fusion.2
  48.1 0.1 multiply_bitcast_fusion
  48.1 0.1 multiply_exponential_fusion
  48.2 0.0 copy-start.3
  48.2 0.0 copy-start.5
  48.3 6.8 %fusion = f32[8,61,16,128]{3,1,2,0:T(8,128)S(1)} fusion(f32[16,61,8,128]{3,2,1,0:T(8,128)} %bitcast.41, f32[8,61,61,1]{2,1,0,3:T(8,128)S(1)} %reshape.171), kind=kOutput, calls=%fused_computation.8 | convolution fusion | flops 731578368 | bytes 8114464 | tf_op jit(solution)/shard_map/nkj,bjnl->bknl/dot_general | solution.py:45
  55.1 0.0 copy-done.3
  55.1 0.0 copy-done.5
  55.1 0.0 copy-start.4
  55.1 6.4 %multiply_reduce_fusion.1 = (f32[16,8,128]{2,0,1:T(8,128)S(1)}, f32[16,8,128]{2,0,1:T(8,128)S(1)}, f32[16,8,128]{2,0,1:T(8,128)S(1)}) fusion(f32[61,8]{0,1:T(8,128)S(1)} %multiply_bitcast_fusion, f32[16,61,8]{1,0,2:T(8,128)S(1)} %multiply_exponential_fusion, f32[8,61,16,128]{3,1,2,0:T(8,128)S(1)} %fusion, f32[16,61,8,128]{3,2,1,0:T(8,128)S(1)} %bitcast.51, ...), kind=kOutput, calls=%fused_computation.13 | convolution fusion | flops 739524608 | bytes 8346208 | tf_op jit(solution)/shard_map/binl,nik->bknl/dot_general | solution.py:44
  61.5 0.1 multiply_reduce_fusion.3
  61.6 0.0 copy-done.4
  61.6 0.2 fusion.6
  61.8 0.1 reshape.87
  61.9 0.1 reshape.174
  62.0 6.7 %all_to_all.20 = f32[4,1,2048]{2,1,0:T(1,128)S(1)} all-to-all(f32[4,1,2048]{2,1,0:T(1,128)S(1)} %reshape.174), channel_id=1, replica_groups=mesh['site'=64,'dom'=4] {'dom'}, dimensions={0} | all-to-all | bytes 65536 | tf_op jit(solution)/shard_map/all_to_all | solution.py:29
  68.7 0.5 broadcast.90
  69.2 0.7 reduce.4
  69.9 0.1 reshape.175
  70.1 0.1 broadcast_in_dim.10
  70.2 1.4 %reshape.176 = f32[64,1,2048]{2,1,0:T(1,128)} reshape(f32[64,2,16,64]{3,2,1,0:T(8,128)S(1)} %broadcast_in_dim.10) | data formatting | bytes 1048576
  71.6 17.0 %all-to-all-start.2 = ((f32[64,1,2048]{2,1,0:T(1,128)}), f32[64,1,2048]{2,1,0:T(1,128)S(1)}, u32[]{:S(2)}, u32[]{:S(2)}) async-start(f32[64,1,2048]{2,1,0:T(1,128)} %reshape.176), calls=%async_computation.2 | async-start | bytes 1048576 | tf_op jit(solution)/shard_map/all_to_all | solution.py:35
  88.7 17.6 %all-to-all-done.2 = f32[64,1,2048]{2,1,0:T(1,128)S(1)} async-done(((f32[64,1,2048]{2,1,0:T(1,128)}), f32[64,1,2048]{2,1,0:T(1,128)S(1)}, u32[]{:S(2)}, u32[]{:S(2)}) %all-to-all-start.2) | async-done | bytes 524320 | tf_op jit(solution)/shard_map/all_to_all | solution.py:35
  106.4 2.8 %reduce.5 = f32[64,2048]{1,0:T(8,128)} reduce(f32[64,1,2048]{2,1,0:T(1,128)S(1)} %all-to-all-done.2, f32[]{:T(128)} %broadcast.90), dimensions={1}, to_apply=%all_to_all.14.reduce_sub_computation | reduce | bytes 1048580 | tf_op jit(solution)/shard_map/all_to_all | solution.py:35
  109.2 1.5 %reshape.177 = f32[64,2,16,64]{3,2,1,0:T(8,128)S(1)} reshape(f32[64,2048]{1,0:T(8,128)} %reduce.5) | data formatting | bytes 1048576
  110.6 0.7 fusion.14
  111.3 0.6 broadcast_in_dim.11
  111.9 3.2 %all-to-all-start.3 = ((f32[4,2,16]{2,1,0:T(2,128)}), f32[4,2,16]{2,1,0:T(2,128)S(1)}, u32[]{:S(2)}, u32[]{:S(2)}) async-start(f32[4,2,16]{2,1,0:T(2,128)} %broadcast_in_dim.11), calls=%async_computation.3 | async-start | bytes 8192 | tf_op jit(solution)/shard_map/all_to_all | solution.py:35
  115.2 0.7 copy.73
  115.9 3.4 %all-to-all-done.3 = f32[4,2,16]{2,1,0:T(2,128)S(1)} async-done(((f32[4,2,16]{2,1,0:T(2,128)}), f32[4,2,16]{2,1,0:T(2,128)S(1)}, u32[]{:S(2)}, u32[]{:S(2)}) %all-to-all-start.3) | async-done | bytes 544 | tf_op jit(solution)/shard_map/all_to_all | solution.py:35
  119.3 0.6 scatter_fusion
  120.0 0.0 copy-start.1
  120.0 0.6 copy-done.1
  (13 shorter events, 0.1 us)
Async XLA Ops:
  0.6 12.0 %copy-start = (f32[64,61,61]{2,0,1:T(8,128)S(1)}, f32[64,61,61]{2,0,1:T(8,128)}, u32[]{:S(2)}) copy-start(f32[64,61,61]{2,0,1:T(8,128)} %param.13) | copy-start | bytes 2857732
  18.6 7.0 %copy-start.2 = (f32[64,61]{1,0:T(8,128)S(1)}, f32[64,61]{1,0:T(8,128)}, u32[]{:S(2)}) copy-start(f32[64,61]{1,0:T(8,128)} %param.15) | copy-start | bytes 46852
  31.5 14.8 %all-to-all-start = ((f32[4,8,7565]{2,1,0:T(8,128)}), f32[4,8,7565]{2,1,0:T(8,128)S(1)}, u32[]{:S(2)}, u32[]{:S(2)}) async-start(f32[4,8,7565]{2,1,0:T(8,128)} %concatenate.3), calls=%async_computation | async-start | bytes 1966080 | tf_op jit(solution)/shard_map/all_to_all | solution.py:16
  48.2 6.8 %copy-start.3 = (f32[8,61,61]{2,1,0:T(8,128)S(1)}, f32[8,61,61]{2,1,0:T(8,128)}, u32[]{:S(2)}) copy-start(f32[8,61,61]{2,1,0:T(8,128)} %reduce_sum.131) | copy-start | bytes 357220
  48.2 6.8 %copy-start.5 = (f32[16,61,1,1024]{3,2,1,0:T(1,128)S(1)}, f32[16,61,1,1024]{3,2,1,0:T(1,128)}, u32[]{:S(2)}) copy-start(f32[16,61,1,1024]{3,2,1,0:T(1,128)} %param.11) | copy-start | bytes 11993092
  55.1 6.5 %copy-start.4 = (s32[1,8]{1,0:T(1,128)S(1)}, s32[1,8]{1,0:T(1,128)}, u32[]{:S(2)}) copy-start(s32[1,8]{1,0:T(1,128)} %param.20) | copy-start | bytes 100
  71.6 34.7 %all-to-all-start.2 = ((f32[64,1,2048]{2,1,0:T(1,128)}), f32[64,1,2048]{2,1,0:T(1,128)S(1)}, u32[]{:S(2)}, u32[]{:S(2)}) async-start(f32[64,1,2048]{2,1,0:T(1,128)} %reshape.176), calls=%async_computation.2 | async-start | bytes 1048576 | tf_op jit(solution)/shard_map/all_to_all | solution.py:35
  111.9 7.4 %all-to-all-start.3 = ((f32[4,2,16]{2,1,0:T(2,128)}), f32[4,2,16]{2,1,0:T(2,128)S(1)}, u32[]{:S(2)}, u32[]{:S(2)}) async-start(f32[4,2,16]{2,1,0:T(2,128)} %broadcast_in_dim.11), calls=%async_computation.3 | async-start | bytes 8192 | tf_op jit(solution)/shard_map/all_to_all | solution.py:35
  120.0 0.6 copy-start.1
where the time goes:
time: 122 us; the launch traced here: 121 us
  waiting for transfers between devices  30.3 us (25%)
  local copies, waits for them, and re-layouts  28.6 us (23%)
  starting transfers between devices  23.8 us (20%)
  blocking collectives  15.6 us (13%)
  matrix products  13.4 us (11%)
  other arithmetic  8 us (7%)
    all_to_all x2, waiting for transfers between devices, copy_for_each(): lax.all_to_all(jnp.broadcast_to(x[None], (count, *x.shape)), axis, 0, 0,...  21 us
    all_to_all x2, starting transfers between devices, copy_for_each(): lax.all_to_all(jnp.broadcast_to(x[None], (count, *x.shape)), axis, 0, 0,...  20.3 us
    all_to_all x1, waiting for transfers between devices, in_one_piece(): lax.all_to_all(both, axis, split_axis=split_dim, concat_axis=concat_dim,...  9.27 us
    all_gather x1, blocking collectives, on_device(): wanted = lax.all_gather(block_partition, 'dom', axis=0, tiled=True)  8.94 us
    gather x3, local copies, waits for them, and re-layouts, on_device(): send_right = right_vectors[clipped] * inside[:, :, None, None]  7.01 us
    dot_general x1, matrix products, project(): jnp.einsum('nkj,bjnl->bknl', vec_right, lower, precision=lax.Precision.HI...  6.8 us
    all_to_all x1, blocking collectives, sum_at_owner(): parts = lax.all_to_all(cut_along(x, dim, count), axis, 0, 0, tiled=True)  6.65 us
    dot_general x1, matrix products, project(): jnp.einsum('binl,nik->bknl', scaled, vec_left, precision=lax.Precision.HI...  6.37 us
  transfers between devices with their start and end apart: 3, of which 3 were waited for; matrix products, arithmetic and copies ran while one was open for 2% of the time, Pallas kernels for 0%

commit v1 on v0

v1 whole, which is shorter than its diff:
```python
import functools

import jax
import jax.numpy as jnp
from jax import lax
from jax.experimental import pallas as pl
from jax.experimental.pallas import tpu as pltpu
from jax.sharding import PartitionSpec as P

BLK = 128
STATES = 61
ROWS = 64
BR = 16
F32 = jnp.float32
BF16 = jnp.bfloat16
MESH = pl.DeviceIdType.MESH


def hi_lo(x):
    hi = x.astype(BF16)
    return hi, (x - hi.astype(F32)).astype(BF16)


def three(x):
    hi = x.astype(BF16)
    rest = x - hi.astype(F32)
    mid = rest.astype(BF16)
    return hi, mid, (rest - mid.astype(F32)).astype(BF16)


def dot(a, b, contract):
    return lax.dot_general(a, b, ((contract[0], contract[1]), ((), ())), preferred_element_type=F32)


def step_kernel(
    sizes,
    top_hbm,
    bottom_hbm,
    left_hbm,
    right_hbm,
    decay_hbm,
    weight_hbm,
    rates,
    lengths,
    chosen,
    blocks,
    pattern_hbm,
    loglik_out,
    part_out,
    updated_out,
    top,
    bottom,
    left,
    right,
    decay,
    weight,
    pattern,
    asked,
    send_tab,
    recv_tab,
    likes,
    sums,
    gath,
    zsum,
    local_sem,
    ask_send,
    ask_recv,
    tab_send,
    tab_recv,
    gath_send,
    gath_recv,
    zsum_send,
    zsum_recv,
):
    planes, across, doms, nblk, owned = sizes
    site = lax.axis_index("site")
    me = lax.axis_index("dom")
    plane = site // across
    column = site % across
    group = across * doms
    rank = column * doms + me
    dom_peer = lambda off: lax.rem(me + off, doms)

    def group_peer(off):
        r = lax.rem(rank + off, group)
        return {"site": plane * across + r // doms, "dom": lax.rem(r, doms)}

    def plane_peer(off):
        return {"site": lax.rem(plane + off, planes) * across + column, "dom": me}

    barrier = pltpu.get_barrier_semaphore()

    @pl.loop(1, group)
    def _(off):
        pl.semaphore_signal(barrier, inc=1, device_id=group_peer(off), device_id_type=MESH)

    @pl.loop(1, planes)
    def _(off):
        pl.semaphore_signal(barrier, inc=1, device_id=plane_peer(off), device_id_type=MESH)

    full = STATES * owned
    loads = [
        pltpu.make_async_copy(left_hbm, left.at[pl.ds(0, full)], local_sem.at[0]),
        pltpu.make_async_copy(right_hbm, right.at[pl.ds(0, full)], local_sem.at[1]),
        pltpu.make_async_copy(decay_hbm, decay, local_sem.at[2]),
        pltpu.make_async_copy(weight_hbm, weight, local_sem.at[3]),
        pltpu.make_async_copy(pattern_hbm, pattern, local_sem.at[4]),
        pltpu.make_async_copy(top_hbm, top.at[pl.ds(0, BR * STATES * nblk)], local_sem.at[5]),
        pltpu.make_async_copy(bottom_hbm, bottom.at[pl.ds(0, BR * STATES * nblk)], local_sem.at[6]),
    ]
    for load in loads:
        load.start()
    tail = (ROWS - STATES) * owned
    left[pl.ds(full, tail), :] = jnp.zeros((tail, STATES), F32)
    right[pl.ds(full, tail), :] = jnp.zeros((tail, STATES), F32)
    tail = (ROWS - STATES) * nblk
    top[pl.ds(BR * STATES * nblk, tail), :] = jnp.zeros((tail, BLK), F32)
    bottom[pl.ds(BR * STATES * nblk, tail), :] = jnp.zeros((tail, BLK), F32)

    pl.semaphore_wait(barrier, group + planes - 2)

    def ask(off):
        return pltpu.make_async_remote_copy(
            src_ref=blocks,
            dst_ref=asked.at[off - 1],
            send_sem=ask_send.at[off - 1],
            recv_sem=ask_recv.at[off - 1],
            device_id={"site": site, "dom": dom_peer(off)},
            device_id_type=MESH,
        )

    for off in range(1, doms):
        ask(off).start()

    row_id = lax.broadcasted_iota(jnp.int32, (ROWS, ROWS), 0)

    def entry(part):
        relative = part - me * owned
        inside = jnp.logical_and(relative >= 0, relative < owned).astype(F32)
        at = jnp.clip(relative, 0, owned - 1)
        lv = jnp.pad(left[pl.ds(at, ROWS, stride=owned), :], ((0, 0), (0, ROWS - STATES)))
        rv = jnp.pad(right[pl.ds(at, ROWS, stride=owned), :], ((0, 0), (0, ROWS - STATES)))
        pad = lambda x: jnp.pad(x, ((0, 0), (0, ROWS - STATES)))
        exponent = pad(-decay[pl.ds(at, 1), :] * rates[at])
        state_w = pad(weight[pl.ds(at, 1), :])
        lv = jnp.where(row_id == STATES, exponent, jnp.where(row_id == STATES + 1, state_w, lv))
        return jnp.concatenate([lv, rv], axis=1) * inside

    def tab(off, n):
        return pltpu.make_async_remote_copy(
            src_ref=send_tab.at[off - 1, n],
            dst_ref=recv_tab.at[off - 1, n],
            send_sem=tab_send.at[off - 1, n],
            recv_sem=tab_recv.at[off - 1, n],
            device_id={"site": site, "dom": dom_peer(off)},
            device_id_type=MESH,
        )

    for load in loads[:4]:
        load.wait()
    for off in range(1, doms):
        ask(off).wait_recv()

    @pl.loop(0, nblk)
    def _(n):
        for off in range(1, doms):
            send_tab[off - 1, n] = entry(asked[doms - off - 1, 0, n])
        for off in range(1, doms):
            tab(off, n).start()

    for load in loads[4:]:
        load.wait()

    lane64 = lax.broadcasted_iota(jnp.int32, (ROWS, ROWS), 1)

    @pl.loop(0, nblk)
    def _(n):
        got = entry(blocks[0, n])
        for off in range(1, doms):
            tab(off, n).wait_recv()
            got = got + recv_tab[off - 1, n]
        lv_t = jnp.transpose(got[:, :ROWS])
        exponent = lv_t[:, STATES : STATES + 1]
        state_w = lv_t[:, STATES + 1 : STATES + 2]
        lv_t = jnp.where(lane64 < STATES, lv_t, 0.0)
        lv_hi, lv_lo = hi_lo(lv_t)
        rv_hi, rv_lo = hi_lo(got[:, ROWS:])
        lhs_l = jnp.concatenate([lv_hi, lv_hi, lv_lo], axis=1)
        lhs_r = jnp.concatenate([rv_hi, rv_hi, rv_lo], axis=1)
        expo_b = jnp.broadcast_to(exponent, (ROWS, BLK))
        w_b = jnp.broadcast_to(state_w, (ROWS, BLK))

        def stacked(ref, b, scale):
            x = ref[pl.ds(b * (STATES * nblk) + n, ROWS, stride=nblk), :]
            if scale is not None:
                x = x * scale
            hi, lo = hi_lo(x)
            return jnp.concatenate([hi, lo, hi], axis=0)

        for b in range(0, BR, 2):
            x = jnp.concatenate([stacked(top, b, w_b), stacked(top, b + 1, w_b)], axis=1)
            y = jnp.concatenate([stacked(bottom, b, None), stacked(bottom, b + 1, None)], axis=1)
            joint = dot(lhs_l, x, ((1,), (0,))) * dot(lhs_r, y, ((1,), (0,)))
            for c in range(2):
                time = lengths[chosen[b + c]]
                decayed = joint[:, c * BLK : (c + 1) * BLK] * jnp.exp(expo_b * time)
                for power in range(3):
                    likes[power, pl.ds(b + c, 1), :] = jnp.sum(decayed, axis=0, keepdims=True)
                    if power < 2:
                        decayed = decayed * expo_b
        like0 = likes[0]
        first = likes[1] / like0
        second = likes[2] / like0 - first * first
        sites_w = pattern[pl.ds(n, 1), :].astype(F32)
        loglik_out[n] = sites_w * jnp.log(like0)
        sums[pl.ds(n * 32, BR), :] = sites_w * first
        sums[pl.ds(n * 32 + BR, BR), :] = sites_w * second

    ones = jnp.ones((8, BLK), BF16)
    total = sum(dot(ones, piece, ((1,), (1,))) for piece in three(sums[...]))
    lane_blk = lax.broadcasted_iota(jnp.int32, (1, BLK), 1) // 32
    for g in range(2):
        gath[rank, pl.ds(g, 1), :] = total[0:1, g * BLK : (g + 1) * BLK]
        ids = jnp.zeros((1, BLK), F32)
        for k in range(4):
            ids = jnp.where(lane_blk == k, blocks[0, g * 4 + k].astype(F32), ids)
        gath[rank, pl.ds(2 + g, 1), :] = ids

    def give(off):
        return pltpu.make_async_remote_copy(
            src_ref=gath.at[rank],
            dst_ref=gath.at[rank],
            send_sem=gath_send.at[off],
            recv_sem=gath_recv.at[off],
            device_id=group_peer(off),
            device_id_type=MESH,
        )

    @pl.loop(1, group)
    def _(off):
        give(off).start()

    @pl.loop(1, group)
    def _(off):
        give(off).wait_recv()

    vals = jnp.concatenate([gath[:, 0, :], gath[:, 1, :]], axis=0)
    ids = jnp.concatenate([gath[:, 2, :], gath[:, 3, :]], axis=0)
    local = lax.broadcasted_iota(jnp.int32, (2 * group, BLK), 1)
    mine = jnp.where(local < owned, local + me * owned, -1).astype(F32)
    hot = jnp.concatenate(
        [(ids[:, k * 32 : k * 32 + 1] == mine).astype(F32).astype(BF16) for k in range(4)], axis=1
    )
    vals_t = jnp.transpose(vals)
    spread = dot(
        jnp.concatenate(three(vals_t), axis=1),
        jnp.concatenate([hot, hot, hot], axis=0),
        ((1,), (0,)),
    )
    by_part = sum(spread[k * 32 : (k + 1) * 32, k * BLK : (k + 1) * BLK] for k in range(4))
    lane = lax.broadcasted_iota(jnp.int32, (BR, BLK), 1)
    zsum[plane, 0:BR, :] = jnp.where(
        lane < owned, by_part[:BR], pltpu.roll(by_part[BR:], owned, 1)
    )
    column_sum = jnp.sum(vals, axis=0, keepdims=True)
    all_sum = column_sum
    for k in range(1, 4):
        all_sum = all_sum + pltpu.roll(column_sum, 32 * k, 1)
    zsum[plane, BR : BR + 8, :] = jnp.broadcast_to(all_sum, (8, BLK))

    def pass_on(off):
        return pltpu.make_async_remote_copy(
            src_ref=zsum.at[plane],
            dst_ref=zsum.at[plane],
            send_sem=zsum_send.at[off],
            recv_sem=zsum_recv.at[off],
            device_id=plane_peer(off),
            device_id_type=MESH,
        )

    @pl.loop(1, planes)
    def _(off):
        pass_on(off).start()

    @pl.loop(1, planes)
    def _(off):
        pass_on(off).wait_recv()

    done = jnp.sum(zsum[...], axis=0)
    both = done[:BR]
    part_out[0] = both[:, :owned]
    part_out[1] = pltpu.roll(both, owned, 1)[:, :owned]
    totals = done[BR : BR + 8]
    lane8 = lax.broadcasted_iota(jnp.int32, (8, BLK), 1)
    times = jnp.zeros((8, BLK), F32)
    for b in range(BR):
        times = jnp.where(lane8 == b, lengths[chosen[b]], times)
    updated_out[...] = times - totals / pltpu.roll(totals, BLK - BR, 1)

    for off in range(1, doms):
        ask(off).wait_send()

        @pl.loop(0, nblk)
        def _(n):
            tab(off, n).wait_send()

    @pl.loop(1, group)
    def _(off):
        give(off).wait_send()

    @pl.loop(1, planes)
    def _(off):
        pass_on(off).wait_send()


def on_device(
    sizes,
    top_partial,
    bottom_partial,
    left_vectors,
    right_vectors,
    decay_rates,
    state_weights,
    part_rates,
    branch_lengths,
    pattern_weights,
    block_partition,
    chosen_branches,
):
    planes, across, doms, nblk, owned = sizes
    flat = BR * STATES * nblk
    group = across * doms
    anywhere = pl.BlockSpec(memory_space=pl.ANY)
    scalars = pl.BlockSpec(memory_space=pltpu.SMEM)
    vmem = pl.BlockSpec(memory_space=pltpu.VMEM)
    loglik, share, updated = pl.pallas_call(
        functools.partial(step_kernel, sizes),
        out_shape=(
            jax.ShapeDtypeStruct((nblk, BR, BLK), F32),
            jax.ShapeDtypeStruct((2, BR, owned), F32),
            jax.ShapeDtypeStruct((8, BLK), F32),
        ),
        in_specs=[anywhere] * 6 + [scalars] * 4 + [anywhere],
        out_specs=(vmem, vmem, vmem),
        scratch_shapes=[
            pltpu.VMEM((flat + (ROWS - STATES) * nblk, BLK), F32),
            pltpu.VMEM((flat + (ROWS - STATES) * nblk, BLK), F32),
            pltpu.VMEM((ROWS * owned, STATES), F32),
            pltpu.VMEM((ROWS * owned, STATES), F32),
            pltpu.VMEM((owned, STATES), F32),
            pltpu.VMEM((owned, STATES), F32),
            pltpu.VMEM((nblk, BLK), jnp.int32),
            pltpu.SMEM((doms - 1, 1, nblk), jnp.int32),
            pltpu.VMEM((doms - 1, nblk, ROWS, BLK), F32),
            pltpu.VMEM((doms - 1, nblk, ROWS, BLK), F32),
            pltpu.VMEM((3, BR, BLK), F32),
            pltpu.VMEM((32 * nblk, BLK), F32),
            pltpu.VMEM((group, 4, BLK), F32),
            pltpu.VMEM((planes, BR + 8, BLK), F32),
            pltpu.SemaphoreType.DMA((7,)),
            pltpu.SemaphoreType.DMA((doms - 1,)),
            pltpu.SemaphoreType.DMA((doms - 1,)),
            pltpu.SemaphoreType.DMA((doms - 1, nblk)),
            pltpu.SemaphoreType.DMA((doms - 1, nblk)),
            pltpu.SemaphoreType.DMA((group,)),
            pltpu.SemaphoreType.DMA((group,)),
            pltpu.SemaphoreType.DMA((planes,)),
            pltpu.SemaphoreType.DMA((planes,)),
        ],
        compiler_params=pltpu.CompilerParams(
            collective_id=0, has_side_effects=True, vmem_limit_bytes=40 * 1024 * 1024
        ),
    )(
        top_partial.reshape(BR, STATES, nblk, BLK).reshape(flat, BLK),
        bottom_partial.reshape(BR, STATES, nblk, BLK).reshape(flat, BLK),
        jnp.transpose(left_vectors, (1, 0, 2)).reshape(STATES * owned, STATES),
        jnp.transpose(right_vectors, (1, 0, 2)).reshape(STATES * owned, STATES),
        decay_rates,
        state_weights,
        part_rates,
        branch_lengths,
        chosen_branches,
        block_partition,
        pattern_weights.reshape(nblk, BLK),
    )
    new_lengths = branch_lengths.at[chosen_branches].set(updated[0, :BR])
    loglik = jnp.transpose(loglik, (1, 0, 2)).reshape(BR, 1, nblk * BLK)
    return (loglik, share, new_lengths)


def solution(mesh):
    sites, doms = mesh.shape["site"], mesh.shape["dom"]
    across = 8 if sites % 8 == 0 and sites > 8 else 2
    sizes = (sites // across, across, doms, 8, 256 // doms)
    return jax.shard_map(
        functools.partial(on_device, sizes),
        mesh=mesh,
        in_specs=(
            P(None, None, "dom", "site"),
            P(None, None, "dom", "site"),
            P("dom", None, None),
            P("dom", None, None),
            P("dom", None),
            P("dom", None),
            P("dom"),
            P(),
            P("dom", "site"),
            P("dom", "site"),
            P(),
        ),
        out_specs=(P(None, "dom", "site"), P(None, None, "dom"), P()),
        check_vma=False,
    )
```

time: 122 us -> 55.1 us (0.45)
  Pallas kernels: 0 us -> 39.8 us
  waiting for transfers between devices: 30.3 us -> 0 us
  starting transfers between devices: 23.8 us -> 0 us
  blocking collectives: 15.6 us -> 0 us
  local copies, waits for them, and re-layouts: 28.6 us -> 14.1 us
  matrix products: 13.4 us -> 0 us
  other arithmetic: 8 us -> 0.01 us
    pallas_call x0 -> x1, Pallas kernels: none -> 39.8 us  [on_device(): pl.pallas_call(functools.partial(step_kernel, sizes), out_shape=(jax.Shap...]
    all_to_all x3 -> x0, waiting for transfers between devices: 30.3 us -> none  [the longest x2 21 us: copy_for_each(): lax.all_to_all(jnp.broadcast_to(x[None], (count, *x.shape)), axis, 0, 0,...]
    all_to_all x3 -> x0, starting transfers between devices: 23.8 us -> none  [the longest x2 20.3 us: copy_for_each(): lax.all_to_all(jnp.broadcast_to(x[None], (count, *x.shape)), axis, 0, 0,...]
    gather x11 -> x0, local copies, waits for them, and re-layouts: 17 us -> none  [the longest x3 7.01 us: on_device(): send_right = right_vectors[clipped] * inside[:, :, None, None]]
    dot_general x3 -> x0, matrix products: 13.4 us -> none  [the longest x1 6.8 us: project(): jnp.einsum('nkj,bjnl->bknl', vec_right, lower, precision=lax.Precision.HI...]
    all_gather x1 -> x0, blocking collectives: 8.94 us -> none  [on_device(): wanted = lax.all_gather(block_partition, 'dom', axis=0, tiled=True)]
    unnamed x18 -> x24, local copies, waits for them, and re-layouts: 5.26 us -> 12.8 us
    all_to_all x1 -> x0, blocking collectives: 6.65 us -> none  [sum_at_owner(): parts = lax.all_to_all(cut_along(x, dim, count), axis, 0, 0, tiled=True)]
  transfers between devices with their start and end apart: 3 -> 0, of which waited for: 3 -> 0; matrix products, arithmetic and copies ran while one was open for 2% -> 0% of each run, Pallas kernels for 0% -> 0%
where the time goes in v1:
time: 55.1 us; the launch traced here: 54.7 us
  Pallas kernels  39.8 us (72%)
  local copies, waits for them, and re-layouts  14.1 us (26%)
  between operations  0.68 us (1%)
    pallas_call x1, Pallas kernels, on_device(): pl.pallas_call(functools.partial(step_kernel, sizes), out_shape=(jax.Shap...  39.8 us
    unnamed x24, local copies, waits for them, and re-layouts  12.8 us

profile of v1, /device:TPU:1, one launch (start us, length us, event | category | flops | bytes accessed | tf_op | source)
XLA Modules:
  0.0 54.7 jit_solution(13514139366619237188)
XLA Ops:
  0.6 0.7 %copy.19.lengths = f32[1997]{0:T(1024)S(1)} copy(f32[1997]{0:T(1024)} %param.18) | data formatting | bytes 15976
  1.3 0.0 copy-start.1
  1.3 2.1 %copy-done.1 = f32[16,61,1,1024]{3,2,1,0:T(1,128)S(1)} copy-done((f32[16,61,1,1024]{3,2,1,0:T(1,128)S(1)}, f32[16,61,1,1024]{3,2,1,0:T(1,128)}, u32[]{:S(2)}) %copy-start.1) | copy-done | bytes 3997720
  3.5 0.0 copy-start.2
  3.5 2.1 %copy-done.2 = f32[16,61,1,1024]{3,2,1,0:T(1,128)S(1)} copy-done((f32[16,61,1,1024]{3,2,1,0:T(1,128)S(1)}, f32[16,61,1,1024]{3,2,1,0:T(1,128)}, u32[]{:S(2)}) %copy-start.2) | copy-done | bytes 3997720
  5.6 0.0 copy-start.3
  5.6 1.6 %copy-done.3 = f32[64,61,61]{2,0,1:T(8,128)S(1)} copy-done((f32[64,61,61]{2,0,1:T(8,128)S(1)}, f32[64,61,61]{2,0,1:T(8,128)}, u32[]{:S(2)}) %copy-start.3) | copy-done | bytes 952600
  7.2 0.0 copy-start.4
  7.2 1.6 %copy-done.4 = f32[64,61,61]{2,0,1:T(8,128)S(1)} copy-done((f32[64,61,61]{2,0,1:T(8,128)S(1)}, f32[64,61,61]{2,0,1:T(8,128)}, u32[]{:S(2)}) %copy-start.4) | copy-done | bytes 952600
  8.7 0.0 copy-start.5
  8.7 0.8 %copy-done.5 = f32[64,61]{1,0:T(8,128)S(1)} copy-done((f32[64,61]{1,0:T(8,128)S(1)}, f32[64,61]{1,0:T(8,128)}, u32[]{:S(2)}) %copy-start.5) | copy-done | bytes 15640
  9.5 0.0 copy-start.6
  9.5 0.8 %copy-done.6 = f32[64,61]{1,0:T(8,128)S(1)} copy-done((f32[64,61]{1,0:T(8,128)S(1)}, f32[64,61]{1,0:T(8,128)}, u32[]{:S(2)}) %copy-start.6) | copy-done | bytes 15640
  10.2 0.0 copy-start.7
  10.2 0.7 %copy-done.7 = s32[1,1024]{1,0:T(1,128)S(1)} copy-done((s32[1,1024]{1,0:T(1,128)S(1)}, s32[1,1024]{1,0:T(1,128)}, u32[]{:S(2)}) %copy-start.7) | copy-done | bytes 4120
  10.9 0.0 copy-start.8
  10.9 0.7 %copy-done.8 = f32[64]{0:T(128)S(1)} copy-done((f32[64]{0:T(128)S(1)}, f32[64]{0:T(128)}, u32[]{:S(2)}) %copy-start.8) | copy-done | bytes 280
  11.6 0.0 copy-start.9
  11.6 0.7 %copy-done.9 = s32[1,8]{1,0:T(1,128)S(1)} copy-done((s32[1,8]{1,0:T(1,128)S(1)}, s32[1,8]{1,0:T(1,128)}, u32[]{:S(2)}) %copy-start.9) | copy-done | bytes 56
  12.2 0.0 copy-start.10
  12.2 0.7 %copy-done.10 = s32[16]{0:T(128)S(1)} copy-done((s32[16]{0:T(128)S(1)}, s32[16]{0:T(128)}, u32[]{:S(2)}) %copy-start.10) | copy-done | bytes 88
  12.9 39.8 %shard_map.130 = (f32[8,16,128]{2,1,0:T(8,128)S(1)}, f32[2,16,64]{2,1,0:T(8,128)S(1)}, f32[8,128]{1,0:T(8,128)S(1)}) custom-call(f32[7808,128]{1,0:T(8,128)S(1)} %bitcast.13, f32[7808,128]{1,0:T(8,128)S(1)} %bitcast.14, f32[3904,61]{1,0:T(8,128)S(1)} %bitcast.15, f32[3904,61]{1,0:T(8,128)S(1)} %bitcast.16, f32[64,61]{1,0:T(8,128)S(1)} %copy-done.5, ...), custom_call_target="tpu_custom_call" | custom-call | tf_op jit(solution)/shard_map/pallas_call | solution.py:336
  52.7 0.6 %scatter_fusion = f32[1997]{0:T(1024)S(1)} fusion(f32[1997]{0:T(1024)S(1)} %copy.19.lengths, s32[16]{0:T(128)S(1)} %compare_select_fusion, f32[16]{0:T(128)S(1)} %slice_bitcast_fusion), kind=kCustom, calls=%fused_computation | custom fusion | bytes 256 | tf_op jit(solution)/shard_map/scatter | solution.py:386
  53.4 0.0 copy-start
  53.4 0.7 %copy.14 = f32[16,8,128]{2,1,0:T(8,128)} copy(f32[16,8,128]{2,0,1:T(8,128)S(1)} %bitcast.17) | data formatting | bytes 131072 | tf_op jit(solution)/shard_map/transpose | solution.py:387
  54.0 0.6 %copy.20 = f32[2,16,64]{2,1,0:T(8,128)} copy(f32[2,16,64]{2,1,0:T(8,128)S(1)} %get-tuple-element.16) | data formatting | bytes 16384
  54.6 0.0 copy-done
  (2 shorter events, 0.0 us)
Async XLA Ops:
  1.3 2.1 %copy-start.1 = (f32[16,61,1,1024]{3,2,1,0:T(1,128)S(1)}, f32[16,61,1,1024]{3,2,1,0:T(1,128)}, u32[]{:S(2)}) copy-start(f32[16,61,1,1024]{3,2,1,0:T(1,128)} %param.11) | copy-start | bytes 11993092
  3.5 2.1 %copy-start.2 = (f32[16,61,1,1024]{3,2,1,0:T(1,128)S(1)}, f32[16,61,1,1024]{3,2,1,0:T(1,128)}, u32[]{:S(2)}) copy-start(f32[16,61,1,1024]{3,2,1,0:T(1,128)} %param.12) | copy-start | bytes 11993092
  5.6 1.6 %copy-start.3 = (f32[64,61,61]{2,0,1:T(8,128)S(1)}, f32[64,61,61]{2,0,1:T(8,128)}, u32[]{:S(2)}) copy-start(f32[64,61,61]{2,0,1:T(8,128)} %param.13) | copy-start | bytes 2857732
  7.2 1.6 %copy-start.4 = (f32[64,61,61]{2,0,1:T(8,128)S(1)}, f32[64,61,61]{2,0,1:T(8,128)}, u32[]{:S(2)}) copy-start(f32[64,61,61]{2,0,1:T(8,128)} %param.14) | copy-start | bytes 2857732
  8.7 0.8 %copy-start.5 = (f32[64,61]{1,0:T(8,128)S(1)}, f32[64,61]{1,0:T(8,128)}, u32[]{:S(2)}) copy-start(f32[64,61]{1,0:T(8,128)} %decay_hbm.1) | copy-start | bytes 46852
  9.5 0.8 %copy-start.6 = (f32[64,61]{1,0:T(8,128)S(1)}, f32[64,61]{1,0:T(8,128)}, u32[]{:S(2)}) copy-start(f32[64,61]{1,0:T(8,128)} %weight_hbm.1) | copy-start | bytes 46852
  10.2 0.7 %copy-start.7 = (s32[1,1024]{1,0:T(1,128)S(1)}, s32[1,1024]{1,0:T(1,128)}, u32[]{:S(2)}) copy-start(s32[1,1024]{1,0:T(1,128)} %param.19) | copy-start | bytes 12292
  10.9 0.7 %copy-start.8 = (f32[64]{0:T(128)S(1)}, f32[64]{0:T(128)}, u32[]{:S(2)}) copy-start(f32[64]{0:T(128)} %rates.1) | copy-start | bytes 772
  11.6 0.7 %copy-start.9 = (s32[1,8]{1,0:T(1,128)S(1)}, s32[1,8]{1,0:T(1,128)}, u32[]{:S(2)}) copy-start(s32[1,8]{1,0:T(1,128)} %blocks.1) | copy-start | bytes 100
  12.2 0.7 %copy-start.10 = (s32[16]{0:T(128)S(1)}, s32[16]{0:T(128)}, u32[]{:S(2)}) copy-start(s32[16]{0:T(128)} %chosen.1) | copy-start | bytes 196
  53.4 1.3 %copy-start = (f32[1997]{0:T(1024)}, f32[1997]{0:T(1024)S(1)}, u32[]{:S(2)}) copy-start(f32[1997]{0:T(1024)S(1)} %scatter_fusion) | copy-start | bytes 23968

commit v2 on v1

--- a/solution.py
+++ b/solution.py
@@ -40,14 +40,14 @@
     right_hbm,
     decay_hbm,
     weight_hbm,
-    rates,
-    lengths,
-    chosen,
-    blocks,
+    rates_hbm,
+    lengths_hbm,
+    chosen_hbm,
+    blocks_hbm,
     pattern_hbm,
     loglik_out,
     part_out,
-    updated_out,
+    lengths_out,
     top,
     bottom,
     left,
@@ -55,6 +55,11 @@
     decay,
     weight,
     pattern,
+    rates,
+    lengths,
+    chosen,
+    blocks,
+    lengths_v,
     asked,
     send_tab,
     recv_tab,
@@ -79,26 +84,33 @@
     column = site % across
     group = across * doms
     rank = column * doms + me
-    dom_peer = lambda off: lax.rem(me + off, doms)
+    dom_at = [me] + [lax.rem(me + off, doms) for off in range(1, doms)]
+    dom_peer = lambda off: dom_at[off]
+    site_at = [site] + [plane * across + lax.rem(column + off, across) for off in range(1, across)]
+    plane_at = [site] + [lax.rem(plane + off, planes) * across + column for off in range(1, planes)]
 
     def group_peer(off):
-        r = lax.rem(rank + off, group)
-        return {"site": plane * across + r // doms, "dom": lax.rem(r, doms)}
+        return {"site": site_at[off // doms], "dom": dom_at[off % doms]}
 
     def plane_peer(off):
-        return {"site": lax.rem(plane + off, planes) * across + column, "dom": me}
+        return {"site": plane_at[off], "dom": me}
 
     barrier = pltpu.get_barrier_semaphore()
-
-    @pl.loop(1, group)
-    def _(off):
+    far = sorted(range(1, group), key=lambda off: -min(off // doms, across - off // doms))
+    for off in sorted(range(1, planes), key=lambda off: -min(off, planes - off)):
+        pl.semaphore_signal(barrier, inc=1, device_id=plane_peer(off), device_id_type=MESH)
+    for off in far:
         pl.semaphore_signal(barrier, inc=1, device_id=group_peer(off), device_id_type=MESH)
 
-    @pl.loop(1, planes)
-    def _(off):
-        pl.semaphore_signal(barrier, inc=1, device_id=plane_peer(off), device_id_type=MESH)
-
     full = STATES * owned
+    small = [
+        pltpu.make_async_copy(blocks_hbm, blocks, local_sem.at[7]),
+        pltpu.make_async_copy(rates_hbm, rates, local_sem.at[8]),
+        pltpu.make_async_copy(chosen_hbm, chosen, local_sem.at[9]),
+        pltpu.make_async_copy(lengths_hbm, lengths, local_sem.at[10]),
+    ]
+    small.append(pltpu.make_async_copy(lengths_hbm, lengths_v, local_sem.at[11]))
+    small[0].start()
     loads = [
         pltpu.make_async_copy(left_hbm, left.at[pl.ds(0, full)], local_sem.at[0]),
         pltpu.make_async_copy(right_hbm, right.at[pl.ds(0, full)], local_sem.at[1]),
@@ -108,7 +120,7 @@
         pltpu.make_async_copy(top_hbm, top.at[pl.ds(0, BR * STATES * nblk)], local_sem.at[5]),
         pltpu.make_async_copy(bottom_hbm, bottom.at[pl.ds(0, BR * STATES * nblk)], local_sem.at[6]),
     ]
-    for load in loads:
+    for load in loads[:4] + small[1:] + loads[4:]:
         load.start()
     tail = (ROWS - STATES) * owned
     left[pl.ds(full, tail), :] = jnp.zeros((tail, STATES), F32)
@@ -117,6 +129,7 @@
     top[pl.ds(BR * STATES * nblk, tail), :] = jnp.zeros((tail, BLK), F32)
     bottom[pl.ds(BR * STATES * nblk, tail), :] = jnp.zeros((tail, BLK), F32)
 
+    small[0].wait()
     pl.semaphore_wait(barrier, group + planes - 2)
 
     def ask(off):
@@ -156,7 +169,7 @@
             device_id_type=MESH,
         )
 
-    for load in loads[:4]:
+    for load in loads[:4] + small[1:]:
         load.wait()
     for off in range(1, doms):
         ask(off).wait_recv()
@@ -212,7 +225,7 @@
         first = likes[1] / like0
         second = likes[2] / like0 - first * first
         sites_w = pattern[pl.ds(n, 1), :].astype(F32)
-        loglik_out[n] = sites_w * jnp.log(like0)
+        loglik_out[pl.ds(n, BR, stride=nblk), :] = sites_w * jnp.log(like0)
         sums[pl.ds(n * 32, BR), :] = sites_w * first
         sums[pl.ds(n * 32 + BR, BR), :] = sites_w * second
 
@@ -236,12 +249,10 @@
             device_id_type=MESH,
         )
 
-    @pl.loop(1, group)
-    def _(off):
+    for off in range(1, group):
         give(off).start()
 
-    @pl.loop(1, group)
-    def _(off):
+    for off in range(1, group):
         give(off).wait_recv()
 
     vals = jnp.concatenate([gath[:, 0, :], gath[:, 1, :]], axis=0)
@@ -278,12 +289,10 @@
             device_id_type=MESH,
         )
 
-    @pl.loop(1, planes)
-    def _(off):
+    for off in range(1, planes):
         pass_on(off).start()
 
-    @pl.loop(1, planes)
-    def _(off):
+    for off in range(1, planes):
         pass_on(off).wait_recv()
 
     done = jnp.sum(zsum[...], axis=0)
@@ -295,7 +304,16 @@
     times = jnp.zeros((8, BLK), F32)
     for b in range(BR):
         times = jnp.where(lane8 == b, lengths[chosen[b]], times)
-    updated_out[...] = times - totals / pltpu.roll(totals, BLK - BR, 1)
+    updated = times - totals / pltpu.roll(totals, BLK - BR, 1)
+    tree = lengths_v.shape[0]
+    index = lax.broadcasted_iota(jnp.int32, (1, BLK), 1)
+    spots = [jnp.broadcast_to(updated[0:1, b : b + 1], (1, BLK)) for b in range(BR)]
+    for start in range(0, tree, BLK):
+        width = min(BLK, tree - start)
+        new = lengths_v[pl.ds(start, width)].reshape(1, width)
+        for b in range(BR):
+            new = jnp.where(index[:, :width] + start == chosen[b], spots[b][:, :width], new)
+        lengths_out[pl.ds(start, width)] = new.reshape(width)
 
     for off in range(1, doms):
         ask(off).wait_send()
@@ -304,13 +322,23 @@
         def _(n):
             tab(off, n).wait_send()
 
-    @pl.loop(1, group)
-    def _(off):
+    for off in range(1, group):
         give(off).wait_send()
 
-    @pl.loop(1, planes)
-    def _(off):
+    for off in range(1, planes):
         pass_on(off).wait_send()
+
+
+def store_kernel(loglik, share, lengths, loglik_out, share_out, lengths_out, sem):
+    copies = [
+        pltpu.make_async_copy(loglik, loglik_out, sem.at[0]),
+        pltpu.make_async_copy(share, share_out, sem.at[1]),
+        pltpu.make_async_copy(lengths, lengths_out, sem.at[2]),
+    ]
+    for copy in copies:
+        copy.start()
+    for copy in copies:
+        copy.wait()
 
 
 def on_device(
@@ -330,17 +358,17 @@
     planes, across, doms, nblk, owned = sizes
     flat = BR * STATES * nblk
     group = across * doms
-    anywhere = pl.BlockSpec(memory_space=pl.ANY)
-    scalars = pl.BlockSpec(memory_space=pltpu.SMEM)
+    hbm = pl.BlockSpec(memory_space=pltpu.HBM)
+    tree = branch_lengths.shape[0]
     vmem = pl.BlockSpec(memory_space=pltpu.VMEM)
-    loglik, share, updated = pl.pallas_call(
+    loglik, share, lengths = pl.pallas_call(
         functools.partial(step_kernel, sizes),
         out_shape=(
-            jax.ShapeDtypeStruct((nblk, BR, BLK), F32),
+            jax.ShapeDtypeStruct((BR * nblk, BLK), F32),
             jax.ShapeDtypeStruct((2, BR, owned), F32),
-            jax.ShapeDtypeStruct((8, BLK), F32),
+            jax.ShapeDtypeStruct((tree,), F32),
         ),
-        in_specs=[anywhere] * 6 + [scalars] * 4 + [anywhere],
+        in_specs=[hbm] * 11,
         out_specs=(vmem, vmem, vmem),
         scratch_shapes=[
             pltpu.VMEM((flat + (ROWS - STATES) * nblk, BLK), F32),
@@ -350,6 +378,11 @@
             pltpu.VMEM((owned, STATES), F32),
             pltpu.VMEM((owned, STATES), F32),
             pltpu.VMEM((nblk, BLK), jnp.int32),
+            pltpu.SMEM((owned,), F32),
+            pltpu.SMEM((tree,), F32),
+            pltpu.SMEM((BR,), jnp.int32),
+            pltpu.SMEM((1, nblk), jnp.int32),
+            pltpu.VMEM((tree,), F32),
             pltpu.SMEM((doms - 1, 1, nblk), jnp.int32),
             pltpu.VMEM((doms - 1, nblk, ROWS, BLK), F32),
             pltpu.VMEM((doms - 1, nblk, ROWS, BLK), F32),
@@ -357,7 +390,7 @@
             pltpu.VMEM((32 * nblk, BLK), F32),
             pltpu.VMEM((group, 4, BLK), F32),
             pltpu.VMEM((planes, BR + 8, BLK), F32),
-            pltpu.SemaphoreType.DMA((7,)),
+            pltpu.SemaphoreType.DMA((12,)),
             pltpu.SemaphoreType.DMA((doms - 1,)),
             pltpu.SemaphoreType.DMA((doms - 1,)),
             pltpu.SemaphoreType.DMA((doms - 1, nblk)),
@@ -368,7 +401,7 @@
             pltpu.SemaphoreType.DMA((planes,)),
         ],
         compiler_params=pltpu.CompilerParams(
-            collective_id=0, has_side_effects=True, vmem_limit_bytes=40 * 1024 * 1024
+            collective_id=0, has_side_effects=True
         ),
     )(
         top_partial.reshape(BR, STATES, nblk, BLK).reshape(flat, BLK),
@@ -383,9 +416,18 @@
         block_partition,
         pattern_weights.reshape(nblk, BLK),
     )
-    new_lengths = branch_lengths.at[chosen_branches].set(updated[0, :BR])
-    loglik = jnp.transpose(loglik, (1, 0, 2)).reshape(BR, 1, nblk * BLK)
-    return (loglik, share, new_lengths)
+    loglik, share, new_lengths = pl.pallas_call(
+        store_kernel,
+        out_shape=(
+            jax.ShapeDtypeStruct((BR * nblk, BLK), F32),
+            jax.ShapeDtypeStruct((2, BR, owned), F32),
+            jax.ShapeDtypeStruct((tree,), F32),
+        ),
+        in_specs=[vmem] * 3,
+        out_specs=(hbm, hbm, hbm),
+        scratch_shapes=[pltpu.SemaphoreType.DMA((3,))],
+    )(loglik, share, lengths)
+    return (loglik.reshape(BR, 1, nblk * BLK), share, new_lengths)
 
 
 def solution(mesh):

time: 55.1 us -> 42 us (0.76)
  local copies, waits for them, and re-layouts: 14.1 us -> 0 us
  Pallas kernels: 39.8 us -> 41.3 us
    unnamed x24 -> x0, local copies, waits for them, and re-layouts: 12.8 us -> none
    pallas_call x0 -> x1, Pallas kernels: none -> 1.52 us  [on_device(): pl.pallas_call(store_kernel, out_shape=(jax.ShapeDtypeStruct((BR * nblk,...]
    transpose x1 -> x0, local copies, waits for them, and re-layouts: 0.65 us -> none  [on_device(): loglik = jnp.transpose(loglik, (1, 0, 2)).reshape(BR, 1, nblk * BLK)]
    scatter x1 -> x0, local copies, waits for them, and re-layouts: 0.65 us -> none  [on_device(): new_lengths = branch_lengths.at[chosen_branches].set(updated[0, :BR])]
where the time goes in v2:
time: 42 us; the launch traced here: 41.9 us
  Pallas kernels  41.3 us (98%)
  between operations  0.64 us (2%)
    pallas_call x1, Pallas kernels, on_device(): pl.pallas_call(functools.partial(step_kernel, sizes), out_shape=(jax.Shap...  39.8 us
    pallas_call x1, Pallas kernels, on_device(): pl.pallas_call(store_kernel, out_shape=(jax.ShapeDtypeStruct((BR * nblk,...  1.52 us

profile of v2, /device:TPU:1, one launch (start us, length us, event | category | flops | bytes accessed | tf_op | source)
XLA Modules:
  0.0 41.9 jit_solution(5213073171729969684)
XLA Ops:
  0.6 39.8 %shard_map.130 = (f32[128,128]{1,0:T(8,128)}, f32[2,16,64]{2,1,0:T(8,128)}, f32[1997]{0:T(1024)}) custom-call(f32[7808,128]{1,0:T(8,128)} %bitcast.10, f32[7808,128]{1,0:T(8,128)} %bitcast.11, f32[3904,61]{1,0:T(8,128)} %bitcast.12, f32[3904,61]{1,0:T(8,128)} %bitcast.13, f32[64,61]{1,0:T(8,128)} %decay_hbm.1, f32[64,61]{1,0:T(8,128)} %weight_hbm.1, ...), custom_call_target="tpu_custom_call" | custom-call | tf_op jit(solution)/shard_map/pallas_call | solution.py:364
  40.4 1.5 %shard_map.131 = (f32[128,128]{1,0:T(8,128)}, f32[2,16,64]{2,1,0:T(8,128)}, f32[1997]{0:T(1024)}) custom-call(f32[128,128]{1,0:T(8,128)} %get-tuple-element.9.loglik, f32[2,16,64]{2,1,0:T(8,128)} %get-tuple-element.10.share, f32[1997]{0:T(1024)} %get-tuple-element.11.lengths), custom_call_target="tpu_custom_call" | custom-call | tf_op jit(solution)/shard_map/pallas_call | solution.py:419

commit v3 on v2

--- a/solution.py
+++ b/solution.py
@@ -48,8 +48,14 @@
     loglik_out,
     part_out,
     lengths_out,
+    loglik_v,
+    part_v,
+    new_v,
     top,
     bottom,
+    top_s,
+    bottom_s,
+    own_tab,
     left,
     right,
     decay,
@@ -61,8 +67,10 @@
     blocks,
     lengths_v,
     asked,
-    send_tab,
+    near_tab,
+    far_tab,
     recv_tab,
+    relay,
     likes,
     sums,
     gath,
@@ -70,12 +78,17 @@
     local_sem,
     ask_send,
     ask_recv,
-    tab_send,
-    tab_recv,
+    near_send,
+    near_recv,
+    far_send,
+    far_recv,
     gath_send,
     gath_recv,
     zsum_send,
     zsum_recv,
+    line_sem,
+    next_sem,
+    after_sem,
 ):
     planes, across, doms, nblk, owned = sizes
     site = lax.axis_index("site")
@@ -95,14 +108,6 @@
     def plane_peer(off):
         return {"site": plane_at[off], "dom": me}
 
-    barrier = pltpu.get_barrier_semaphore()
-    far = sorted(range(1, group), key=lambda off: -min(off // doms, across - off // doms))
-    for off in sorted(range(1, planes), key=lambda off: -min(off, planes - off)):
-        pl.semaphore_signal(barrier, inc=1, device_id=plane_peer(off), device_id_type=MESH)
-    for off in far:
-        pl.semaphore_signal(barrier, inc=1, device_id=group_peer(off), device_id_type=MESH)
-
-    full = STATES * owned
     small = [
         pltpu.make_async_copy(blocks_hbm, blocks, local_sem.at[7]),
         pltpu.make_async_copy(rates_hbm, rates, local_sem.at[8]),
@@ -112,8 +117,8 @@
     small.append(pltpu.make_async_copy(lengths_hbm, lengths_v, local_sem.at[11]))
     small[0].start()
     loads = [
-        pltpu.make_async_copy(left_hbm, left.at[pl.ds(0, full)], local_sem.at[0]),
-        pltpu.make_async_copy(right_hbm, right.at[pl.ds(0, full)], local_sem.at[1]),
+        pltpu.make_async_copy(left_hbm, left.at[pl.ds(0, STATES), pl.ds(0, owned)], local_sem.at[0]),
+        pltpu.make_async_copy(right_hbm, right.at[pl.ds(0, STATES), pl.ds(0, owned)], local_sem.at[1]),
         pltpu.make_async_copy(decay_hbm, decay, local_sem.at[2]),
         pltpu.make_async_copy(weight_hbm, weight, local_sem.at[3]),
         pltpu.make_async_copy(pattern_hbm, pattern, local_sem.at[4]),
@@ -122,15 +127,25 @@
     ]
     for load in loads[:4] + small[1:] + loads[4:]:
         load.start()
-    tail = (ROWS - STATES) * owned
-    left[pl.ds(full, tail), :] = jnp.zeros((tail, STATES), F32)
-    right[pl.ds(full, tail), :] = jnp.zeros((tail, STATES), F32)
+
+    barrier = pltpu.get_barrier_semaphore()
+    here = lambda s: {"site": s, "dom": me}
+    near = [{"site": site, "dom": d} for d in dom_at[1:]]
+    near += [here(s) for s in site_at[1:]] + [here(plane_at[1]), here(plane_at[planes - 1])]
+    for device in near:
+        pl.semaphore_signal(barrier, inc=1, device_id=device, device_id_type=MESH)
+    pitch = left.shape[1]
+    tail = (ROWS - STATES, pitch, STATES)
+    left[pl.ds(STATES, ROWS - STATES)] = jnp.zeros(tail, F32)
+    right[pl.ds(STATES, ROWS - STATES)] = jnp.zeros(tail, F32)
+    left_rows = left.reshape(ROWS * pitch, STATES)
+    right_rows = right.reshape(ROWS * pitch, STATES)
     tail = (ROWS - STATES) * nblk
     top[pl.ds(BR * STATES * nblk, tail), :] = jnp.zeros((tail, BLK), F32)
     bottom[pl.ds(BR * STATES * nblk, tail), :] = jnp.zeros((tail, BLK), F32)
 
     small[0].wait()
-    pl.semaphore_wait(barrier, group + planes - 2)
+    pl.semaphore_wait(barrier, len(near))
 
     def ask(off):
         return pltpu.make_async_remote_copy(
@@ -145,78 +160,144 @@
     for off in range(1, doms):
         ask(off).start()
 
+    for s in site_at[1:]:
+        pl.semaphore_signal(line_sem, inc=1, device_id=here(s), device_id_type=MESH)
+    for off in (1, planes - 1):
+        pl.semaphore_signal(next_sem, inc=1, device_id=here(plane_at[off]), device_id_type=MESH)
+
     row_id = lax.broadcasted_iota(jnp.int32, (ROWS, ROWS), 0)
 
     def entry(part):
         relative = part - me * owned
         inside = jnp.logical_and(relative >= 0, relative < owned).astype(F32)
         at = jnp.clip(relative, 0, owned - 1)
-        lv = jnp.pad(left[pl.ds(at, ROWS, stride=owned), :], ((0, 0), (0, ROWS - STATES)))
-        rv = jnp.pad(right[pl.ds(at, ROWS, stride=owned), :], ((0, 0), (0, ROWS - STATES)))
+        lv = jnp.pad(left_rows[pl.ds(at, ROWS, stride=pitch), :], ((0, 0), (0, ROWS - STATES)))
+        rv = jnp.pad(right_rows[pl.ds(at, ROWS, stride=pitch), :], ((0, 0), (0, ROWS - STATES)))
         pad = lambda x: jnp.pad(x, ((0, 0), (0, ROWS - STATES)))
         exponent = pad(-decay[pl.ds(at, 1), :] * rates[at])
         state_w = pad(weight[pl.ds(at, 1), :])
         lv = jnp.where(row_id == STATES, exponent, jnp.where(row_id == STATES + 1, state_w, lv))
         return jnp.concatenate([lv, rv], axis=1) * inside
 
-    def tab(off, n):
+    half = nblk // 2
+    to_side = [dom_at[doms - 1], dom_at[1]]
+    near_ids, far_ids = [0, doms - 2], 1
+
+    def near(side, n):
         return pltpu.make_async_remote_copy(
-            src_ref=send_tab.at[off - 1, n],
-            dst_ref=recv_tab.at[off - 1, n],
-            send_sem=tab_send.at[off - 1, n],
-            recv_sem=tab_recv.at[off - 1, n],
-            device_id={"site": site, "dom": dom_peer(off)},
+            src_ref=near_tab.at[side, n],
+            dst_ref=recv_tab.at[side, n],
+            send_sem=near_send.at[side, n],
+            recv_sem=near_recv.at[side, n],
+            device_id={"site": site, "dom": to_side[side]},
             device_id_type=MESH,
         )
 
+    def far(side, i):
+        return pltpu.make_async_remote_copy(
+            src_ref=far_tab.at[side, i],
+            dst_ref=relay.at[side, i],
+            send_sem=far_send.at[side, i],
+            recv_sem=far_recv.at[side, i],
+            device_id={"site": site, "dom": to_side[side]},
+            device_id_type=MESH,
+        )
+
+    def direct(start, stop):
+        @pl.loop(start, stop)
+        def _(i):
+            for side in range(2):
+                n = (1 - side) * half + i
+                near_tab[side, n] = entry(asked[near_ids[side], 0, n])
+            for side in range(2):
+                near(side, (1 - side) * half + i).start()
+
+    def split(ref, out):
+        @pl.loop(0, nblk)
+        def _(n):
+            for b in range(BR):
+                hi, lo = hi_lo(ref[pl.ds(b * (STATES * nblk) + n, ROWS, stride=nblk), :])
+                lanes = pl.ds((b % 2) * BLK, BLK)
+                out[n, b // 2, pl.ds(0, ROWS), lanes] = hi
+                out[n, b // 2, pl.ds(ROWS, ROWS), lanes] = lo
+
+    def passed_on(start, stop):
+        @pl.loop(start, stop)
+        def _(i):
+            for side in range(2):
+                n = side * half + i
+                mine = entry(asked[near_ids[side], 0, n])
+                far(side, i).wait_recv()
+                near_tab[side, n] = mine + relay[side, i]
+            for side in range(2):
+                near(side, side * half + i).start()
+
     for load in loads[:4] + small[1:]:
         load.wait()
+    loads[4].wait()
+    loads[5].wait()
+    split(top, top_s)
     for off in range(1, doms):
         ask(off).wait_recv()
 
+    @pl.loop(0, half)
+    def _(i):
+        for side in range(2):
+            far_tab[side, i] = entry(asked[far_ids, 0, side * half + i])
+        for side in range(2):
+            far(side, i).start()
+
+    direct(0, half - 2)
+
     @pl.loop(0, nblk)
     def _(n):
-        for off in range(1, doms):
-            send_tab[off - 1, n] = entry(asked[doms - off - 1, 0, n])
-        for off in range(1, doms):
-            tab(off, n).start()
-
-    for load in loads[4:]:
-        load.wait()
-
+        own_tab[n] = entry(blocks[0, n])
+
+    loads[6].wait()
+    split(bottom, bottom_s)
+    passed_on(0, 1)
+    direct(half - 2, half - 1)
+    passed_on(1, 2)
+    direct(half - 1, half)
+    passed_on(2, half)
+
+    pl.semaphore_wait(next_sem, 2)
+    for off in (2, planes - 2):
+        pl.semaphore_signal(after_sem, inc=1, device_id=here(plane_at[off]), device_id_type=MESH)
+
+    lane1 = lax.broadcasted_iota(jnp.int32, (1, BLK), 1)
+    times = jnp.zeros((1, BLK), F32)
+    for b in range(BR):
+        times = jnp.where(lane1 == b, lengths[chosen[b]], times)
     lane64 = lax.broadcasted_iota(jnp.int32, (ROWS, ROWS), 1)
 
     @pl.loop(0, nblk)
-    def _(n):
-        got = entry(blocks[0, n])
-        for off in range(1, doms):
-            tab(off, n).wait_recv()
-            got = got + recv_tab[off - 1, n]
+    def _(turn):
+        n = (turn % 2) * half + turn // 2
+        got = own_tab[n]
+        for side in range(2):
+            near(side, n).wait_recv()
+            got = got + recv_tab[side, n]
         lv_t = jnp.transpose(got[:, :ROWS])
+        state_w = got[STATES + 1 : STATES + 2, :ROWS]
         exponent = lv_t[:, STATES : STATES + 1]
-        state_w = lv_t[:, STATES + 1 : STATES + 2]
-        lv_t = jnp.where(lane64 < STATES, lv_t, 0.0)
+        lv_t = jnp.where(lane64 < STATES, lv_t * state_w, 0.0)
         lv_hi, lv_lo = hi_lo(lv_t)
         rv_hi, rv_lo = hi_lo(got[:, ROWS:])
         lhs_l = jnp.concatenate([lv_hi, lv_hi, lv_lo], axis=1)
         lhs_r = jnp.concatenate([rv_hi, rv_hi, rv_lo], axis=1)
         expo_b = jnp.broadcast_to(exponent, (ROWS, BLK))
-        w_b = jnp.broadcast_to(state_w, (ROWS, BLK))
-
-        def stacked(ref, b, scale):
-            x = ref[pl.ds(b * (STATES * nblk) + n, ROWS, stride=nblk), :]
-            if scale is not None:
-                x = x * scale
-            hi, lo = hi_lo(x)
-            return jnp.concatenate([hi, lo, hi], axis=0)
+        decays = jnp.exp(exponent * times)
+
+        def stacked(ref, pair):
+            x = ref[n, pair]
+            return jnp.concatenate([x, x[:ROWS]], axis=0)
 
         for b in range(0, BR, 2):
-            x = jnp.concatenate([stacked(top, b, w_b), stacked(top, b + 1, w_b)], axis=1)
-            y = jnp.concatenate([stacked(bottom, b, None), stacked(bottom, b + 1, None)], axis=1)
+            x, y = stacked(top_s, b // 2), stacked(bottom_s, b // 2)
             joint = dot(lhs_l, x, ((1,), (0,))) * dot(lhs_r, y, ((1,), (0,)))
             for c in range(2):
-                time = lengths[chosen[b + c]]
-                decayed = joint[:, c * BLK : (c + 1) * BLK] * jnp.exp(expo_b * time)
+                decayed = joint[:, c * BLK : (c + 1) * BLK] * decays[:, b + c : b + c + 1]
                 for power in range(3):
                     likes[power, pl.ds(b + c, 1), :] = jnp.sum(decayed, axis=0, keepdims=True)
                     if power < 2:
@@ -225,9 +306,18 @@
         first = likes[1] / like0
         second = likes[2] / like0 - first * first
         sites_w = pattern[pl.ds(n, 1), :].astype(F32)
-        loglik_out[pl.ds(n, BR, stride=nblk), :] = sites_w * jnp.log(like0)
+        loglik_v[pl.ds(n, BR, stride=nblk), :] = sites_w * jnp.log(like0)
         sums[pl.ds(n * 32, BR), :] = sites_w * first
         sums[pl.ds(n * 32 + BR, BR), :] = sites_w * second
+
+    stores = [
+        pltpu.make_async_copy(loglik_v, loglik_out, local_sem.at[12]),
+        pltpu.make_async_copy(part_v, part_out, local_sem.at[13]),
+        pltpu.make_async_copy(new_v, lengths_out, local_sem.at[14]),
+    ]
+    stores[0].start()
+    pl.semaphore_wait(line_sem, across - 1)
+    pl.semaphore_wait(after_sem, 2)
 
     ones = jnp.ones((8, BLK), BF16)
     total = sum(dot(ones, piece, ((1,), (1,))) for piece in three(sums[...]))
@@ -249,7 +339,12 @@
             device_id_type=MESH,
         )
 
-    for off in range(1, group):
+    hops = lambda off, count: min(off, count - off)
+    spread_out = sorted(
+        range(1, group),
+        key=lambda off: -hops(off // doms // 2, across // 2) - hops(off % doms, doms),
+    )
+    for off in spread_out:
         give(off).start()
 
     for off in range(1, group):
@@ -289,7 +384,7 @@
             device_id_type=MESH,
         )
 
-    for off in range(1, planes):
+    for off in sorted(range(1, planes), key=lambda off: -hops(off, planes)):
         pass_on(off).start()
 
     for off in range(1, planes):
@@ -297,13 +392,10 @@
 
     done = jnp.sum(zsum[...], axis=0)
     both = done[:BR]
-    part_out[0] = both[:, :owned]
-    part_out[1] = pltpu.roll(both, owned, 1)[:, :owned]
+    part_v[0] = both[:, :owned]
+    part_v[1] = pltpu.roll(both, owned, 1)[:, :owned]
+    stores[1].start()
     totals = done[BR : BR + 8]
-    lane8 = lax.broadcasted_iota(jnp.int32, (8, BLK), 1)
-    times = jnp.zeros((8, BLK), F32)
-    for b in range(BR):
-        times = jnp.where(lane8 == b, lengths[chosen[b]], times)
     updated = times - totals / pltpu.roll(totals, BLK - BR, 1)
     tree = lengths_v.shape[0]
     index = lax.broadcasted_iota(jnp.int32, (1, BLK), 1)
@@ -313,20 +405,29 @@
         new = lengths_v[pl.ds(start, width)].reshape(1, width)
         for b in range(BR):
             new = jnp.where(index[:, :width] + start == chosen[b], spots[b][:, :width], new)
-        lengths_out[pl.ds(start, width)] = new.reshape(width)
-
+        new_v[pl.ds(start, width)] = new.reshape(width)
+
+    stores[2].start()
     for off in range(1, doms):
         ask(off).wait_send()
 
-        @pl.loop(0, nblk)
-        def _(n):
-            tab(off, n).wait_send()
+    @pl.loop(0, nblk)
+    def _(n):
+        for side in range(2):
+            near(side, n).wait_send()
+
+    @pl.loop(0, half)
+    def _(i):
+        for side in range(2):
+            far(side, i).wait_send()
 
     for off in range(1, group):
         give(off).wait_send()
 
     for off in range(1, planes):
         pass_on(off).wait_send()
+    for store in stores:
+        store.wait()
 
 
 def store_kernel(loglik, share, lengths, loglik_out, share_out, lengths_out, sem):
@@ -360,7 +461,6 @@
     group = across * doms
     hbm = pl.BlockSpec(memory_space=pltpu.HBM)
     tree = branch_lengths.shape[0]
-    vmem = pl.BlockSpec(memory_space=pltpu.VMEM)
     loglik, share, lengths = pl.pallas_call(
         functools.partial(step_kernel, sizes),
         out_shape=(
@@ -369,12 +469,18 @@
             jax.ShapeDtypeStruct((tree,), F32),
         ),
         in_specs=[hbm] * 11,
-        out_specs=(vmem, vmem, vmem),
+        out_specs=(hbm, hbm, hbm),
         scratch_shapes=[
+            pltpu.VMEM((BR * nblk, BLK), F32),
+            pltpu.VMEM((2, BR, owned), F32),
+            pltpu.VMEM((tree,), F32),
             pltpu.VMEM((flat + (ROWS - STATES) * nblk, BLK), F32),
             pltpu.VMEM((flat + (ROWS - STATES) * nblk, BLK), F32),
-            pltpu.VMEM((ROWS * owned, STATES), F32),
-            pltpu.VMEM((ROWS * owned, STATES), F32),
+            pltpu.VMEM((nblk, BR // 2, 2 * ROWS, 2 * BLK), BF16),
+            pltpu.VMEM((nblk, BR // 2, 2 * ROWS, 2 * BLK), BF16),
+            pltpu.VMEM((nblk, ROWS, BLK), F32),
+            pltpu.VMEM((ROWS, owned + 8, STATES), F32),
+            pltpu.VMEM((ROWS, owned + 8, STATES), F32),
             pltpu.VMEM((owned, STATES), F32),
             pltpu.VMEM((owned, STATES), F32),
             pltpu.VMEM((nblk, BLK), jnp.int32),
@@ -384,21 +490,28 @@
             pltpu.SMEM((1, nblk), jnp.int32),
             pltpu.VMEM((tree,), F32),
             pltpu.SMEM((doms - 1, 1, nblk), jnp.int32),
-            pltpu.VMEM((doms - 1, nblk, ROWS, BLK), F32),
-            pltpu.VMEM((doms - 1, nblk, ROWS, BLK), F32),
+            pltpu.VMEM((2, nblk, ROWS, BLK), F32),
+            pltpu.VMEM((2, nblk // 2, ROWS, BLK), F32),
+            pltpu.VMEM((2, nblk, ROWS, BLK), F32),
+            pltpu.VMEM((2, nblk // 2, ROWS, BLK), F32),
             pltpu.VMEM((3, BR, BLK), F32),
             pltpu.VMEM((32 * nblk, BLK), F32),
             pltpu.VMEM((group, 4, BLK), F32),
             pltpu.VMEM((planes, BR + 8, BLK), F32),
-            pltpu.SemaphoreType.DMA((12,)),
+            pltpu.SemaphoreType.DMA((15,)),
             pltpu.SemaphoreType.DMA((doms - 1,)),
             pltpu.SemaphoreType.DMA((doms - 1,)),
-            pltpu.SemaphoreType.DMA((doms - 1, nblk)),
-            pltpu.SemaphoreType.DMA((doms - 1, nblk)),
+            pltpu.SemaphoreType.DMA((2, nblk)),
+            pltpu.SemaphoreType.DMA((2, nblk)),
+            pltpu.SemaphoreType.DMA((2, nblk // 2)),
+            pltpu.SemaphoreType.DMA((2, nblk // 2)),
             pltpu.SemaphoreType.DMA((group,)),
             pltpu.SemaphoreType.DMA((group,)),
             pltpu.SemaphoreType.DMA((planes,)),
             pltpu.SemaphoreType.DMA((planes,)),
+            pltpu.SemaphoreType.REGULAR,
+            pltpu.SemaphoreType.REGULAR,
+            pltpu.SemaphoreType.REGULAR,
         ],
         compiler_params=pltpu.CompilerParams(
             collective_id=0, has_side_effects=True
@@ -406,8 +519,8 @@
     )(
         top_partial.reshape(BR, STATES, nblk, BLK).reshape(flat, BLK),
         bottom_partial.reshape(BR, STATES, nblk, BLK).reshape(flat, BLK),
-        jnp.transpose(left_vectors, (1, 0, 2)).reshape(STATES * owned, STATES),
-        jnp.transpose(right_vectors, (1, 0, 2)).reshape(STATES * owned, STATES),
+        jnp.transpose(left_vectors, (1, 0, 2)),
+        jnp.transpose(right_vectors, (1, 0, 2)),
         decay_rates,
         state_weights,
         part_rates,
@@ -423,7 +536,7 @@
             jax.ShapeDtypeStruct((2, BR, owned), F32),
             jax.ShapeDtypeStruct((tree,), F32),
         ),
-        in_specs=[vmem] * 3,
+        in_specs=[pl.BlockSpec(memory_space=pltpu.VMEM)] * 3,
         out_specs=(hbm, hbm, hbm),
         scratch_shapes=[pltpu.SemaphoreType.DMA((3,))],
     )(loglik, share, lengths)

time: 42 us -> 39.6 us (0.943)
  Pallas kernels: 41.3 us -> 38.8 us
    pallas_call x1, Pallas kernels: 39.8 us -> 37.3 us  [on_device(): pl.pallas_call(functools.partial(step_kernel, sizes), out_shape=(jax.Shap...]
where the time goes in v3:
time: 39.6 us; the launch traced here: 39.5 us
  Pallas kernels  38.8 us (98%)
  between operations  0.64 us (2%)
    pallas_call x1, Pallas kernels, on_device(): pl.pallas_call(functools.partial(step_kernel, sizes), out_shape=(jax.Shap...  37.3 us
    pallas_call x1, Pallas kernels, on_device(): pl.pallas_call(store_kernel, out_shape=(jax.ShapeDtypeStruct((BR * nblk,...  1.52 us

profile of v3, /device:TPU:1, one launch (start us, length us, event | category | flops | bytes accessed | tf_op | source)
XLA Modules:
  0.0 39.5 jit_solution(10099601927244680715)
XLA Ops:
  0.6 37.3 %shard_map.130 = (f32[128,128]{1,0:T(8,128)}, f32[2,16,64]{2,1,0:T(8,128)}, f32[1997]{0:T(1024)}) custom-call(f32[7808,128]{1,0:T(8,128)} %bitcast.6, f32[7808,128]{1,0:T(8,128)} %bitcast.7, f32[61,64,61]{2,1,0:T(8,128)} %bitcast.8, f32[61,64,61]{2,1,0:T(8,128)} %bitcast.9, f32[64,61]{1,0:T(8,128)} %decay_hbm.1, f32[64,61]{1,0:T(8,128)} %weight_hbm.1, ...), custom_call_target="tpu_custom_call" | custom-call | tf_op jit(solution)/shard_map/pallas_call | solution.py:464
  38.0 1.5 %shard_map.131 = (f32[128,128]{1,0:T(8,128)}, f32[2,16,64]{2,1,0:T(8,128)}, f32[1997]{0:T(1024)}) custom-call(f32[128,128]{1,0:T(8,128)} %get-tuple-element.9.loglik, f32[2,16,64]{2,1,0:T(8,128)} %get-tuple-element.10.share, f32[1997]{0:T(1024)} %get-tuple-element.11.lengths), custom_call_target="tpu_custom_call" | custom-call | tf_op jit(solution)/shard_map/pallas_call | solution.py:532

commit v4 on v3

--- a/solution.py
+++ b/solution.py
@@ -97,6 +97,9 @@
     column = site % across
     group = across * doms
     rank = column * doms + me
+    def wait_for(ref, sem):
+        pltpu.make_async_copy(ref, ref, sem).wait()
+
     dom_at = [me] + [lax.rem(me + off, doms) for off in range(1, doms)]
     dom_peer = lambda off: dom_at[off]
     site_at = [site] + [plane * across + lax.rem(column + off, across) for off in range(1, across)]
@@ -134,6 +137,23 @@
     near += [here(s) for s in site_at[1:]] + [here(plane_at[1]), here(plane_at[planes - 1])]
     for device in near:
         pl.semaphore_signal(barrier, inc=1, device_id=device, device_id_type=MESH)
+
+    small[0].wait()
+    pl.semaphore_wait(barrier, len(near))
+
+    def ask(off):
+        return pltpu.make_async_remote_copy(
+            src_ref=blocks,
+            dst_ref=asked.at[off - 1],
+            send_sem=ask_send,
+            recv_sem=ask_recv.at[off - 1],
+            device_id={"site": site, "dom": dom_peer(off)},
+            device_id_type=MESH,
+        )
+
+    for off in range(1, doms):
+        ask(off).start()
+
     pitch = left.shape[1]
     tail = (ROWS - STATES, pitch, STATES)
     left[pl.ds(STATES, ROWS - STATES)] = jnp.zeros(tail, F32)
@@ -143,22 +163,6 @@
     tail = (ROWS - STATES) * nblk
     top[pl.ds(BR * STATES * nblk, tail), :] = jnp.zeros((tail, BLK), F32)
     bottom[pl.ds(BR * STATES * nblk, tail), :] = jnp.zeros((tail, BLK), F32)
-
-    small[0].wait()
-    pl.semaphore_wait(barrier, len(near))
-
-    def ask(off):
-        return pltpu.make_async_remote_copy(
-            src_ref=blocks,
-            dst_ref=asked.at[off - 1],
-            send_sem=ask_send.at[off - 1],
-            recv_sem=ask_recv.at[off - 1],
-            device_id={"site": site, "dom": dom_peer(off)},
-            device_id_type=MESH,
-        )
-
-    for off in range(1, doms):
-        ask(off).start()
 
     for s in site_at[1:]:
         pl.semaphore_signal(line_sem, inc=1, device_id=here(s), device_id_type=MESH)
@@ -187,8 +191,8 @@
         return pltpu.make_async_remote_copy(
             src_ref=near_tab.at[side, n],
             dst_ref=recv_tab.at[side, n],
-            send_sem=near_send.at[side, n],
-            recv_sem=near_recv.at[side, n],
+            send_sem=near_send,
+            recv_sem=near_recv.at[n],
             device_id={"site": site, "dom": to_side[side]},
             device_id_type=MESH,
         )
@@ -197,8 +201,8 @@
         return pltpu.make_async_remote_copy(
             src_ref=far_tab.at[side, i],
             dst_ref=relay.at[side, i],
-            send_sem=far_send.at[side, i],
-            recv_sem=far_recv.at[side, i],
+            send_sem=far_send,
+            recv_sem=far_recv.at[i],
             device_id={"site": site, "dom": to_side[side]},
             device_id_type=MESH,
         )
@@ -224,11 +228,10 @@
     def passed_on(start, stop):
         @pl.loop(start, stop)
         def _(i):
+            mine = [entry(asked[near_ids[side], 0, side * half + i]) for side in range(2)]
+            wait_for(relay.at[:, i], far_recv.at[i])
             for side in range(2):
-                n = side * half + i
-                mine = entry(asked[near_ids[side], 0, n])
-                far(side, i).wait_recv()
-                near_tab[side, n] = mine + relay[side, i]
+                near_tab[side, side * half + i] = mine[side] + relay[side, i]
             for side in range(2):
                 near(side, side * half + i).start()
 
@@ -271,12 +274,9 @@
         times = jnp.where(lane1 == b, lengths[chosen[b]], times)
     lane64 = lax.broadcasted_iota(jnp.int32, (ROWS, ROWS), 1)
 
-    @pl.loop(0, nblk)
-    def _(turn):
-        n = (turn % 2) * half + turn // 2
+    def one_block(n, slot):
         got = own_tab[n]
         for side in range(2):
-            near(side, n).wait_recv()
             got = got + recv_tab[side, n]
         lv_t = jnp.transpose(got[:, :ROWS])
         state_w = got[STATES + 1 : STATES + 2, :ROWS]
@@ -299,16 +299,23 @@
             for c in range(2):
                 decayed = joint[:, c * BLK : (c + 1) * BLK] * decays[:, b + c : b + c + 1]
                 for power in range(3):
-                    likes[power, pl.ds(b + c, 1), :] = jnp.sum(decayed, axis=0, keepdims=True)
+                    likes[slot, power, pl.ds(b + c, 1), :] = jnp.sum(decayed, axis=0, keepdims=True)
                     if power < 2:
                         decayed = decayed * expo_b
-        like0 = likes[0]
-        first = likes[1] / like0
-        second = likes[2] / like0 - first * first
+        like0, like1, like2 = (likes[slot, power] for power in range(3))
+        first = like1 / like0
+        second = like2 / like0 - first * first
         sites_w = pattern[pl.ds(n, 1), :].astype(F32)
         loglik_v[pl.ds(n, BR, stride=nblk), :] = sites_w * jnp.log(like0)
         sums[pl.ds(n * 32, BR), :] = sites_w * first
         sums[pl.ds(n * 32 + BR, BR), :] = sites_w * second
+
+    @pl.loop(0, half)
+    def _(i):
+        for side in range(2):
+            wait_for(recv_tab.at[:, side * half + i], near_recv.at[side * half + i])
+        for side in range(2):
+            one_block(side * half + i, side)
 
     stores = [
         pltpu.make_async_copy(loglik_v, loglik_out, local_sem.at[12]),
@@ -333,8 +340,8 @@
         return pltpu.make_async_remote_copy(
             src_ref=gath.at[rank],
             dst_ref=gath.at[rank],
-            send_sem=gath_send.at[off],
-            recv_sem=gath_recv.at[off],
+            send_sem=gath_send,
+            recv_sem=gath_recv,
             device_id=group_peer(off),
             device_id_type=MESH,
         )
@@ -347,8 +354,7 @@
     for off in spread_out:
         give(off).start()
 
-    for off in range(1, group):
-        give(off).wait_recv()
+    wait_for(gath.at[pl.ds(0, group - 1)], gath_recv)
 
     vals = jnp.concatenate([gath[:, 0, :], gath[:, 1, :]], axis=0)
     ids = jnp.concatenate([gath[:, 2, :], gath[:, 3, :]], axis=0)
@@ -372,14 +378,14 @@
     all_sum = column_sum
     for k in range(1, 4):
         all_sum = all_sum + pltpu.roll(column_sum, 32 * k, 1)
-    zsum[plane, BR : BR + 8, :] = jnp.broadcast_to(all_sum, (8, BLK))
+    zsum[plane, BR : BR + 1, :] = all_sum
 
     def pass_on(off):
         return pltpu.make_async_remote_copy(
             src_ref=zsum.at[plane],
             dst_ref=zsum.at[plane],
-            send_sem=zsum_send.at[off],
-            recv_sem=zsum_recv.at[off],
+            send_sem=zsum_send,
+            recv_sem=zsum_recv,
             device_id=plane_peer(off),
             device_id_type=MESH,
         )
@@ -387,15 +393,14 @@
     for off in sorted(range(1, planes), key=lambda off: -hops(off, planes)):
         pass_on(off).start()
 
-    for off in range(1, planes):
-        pass_on(off).wait_recv()
+    wait_for(zsum.at[pl.ds(0, planes - 1)], zsum_recv)
 
     done = jnp.sum(zsum[...], axis=0)
     both = done[:BR]
     part_v[0] = both[:, :owned]
     part_v[1] = pltpu.roll(both, owned, 1)[:, :owned]
     stores[1].start()
-    totals = done[BR : BR + 8]
+    totals = jnp.broadcast_to(done[BR : BR + 1], (8, BLK))
     updated = times - totals / pltpu.roll(totals, BLK - BR, 1)
     tree = lengths_v.shape[0]
     index = lax.broadcasted_iota(jnp.int32, (1, BLK), 1)
@@ -408,24 +413,11 @@
         new_v[pl.ds(start, width)] = new.reshape(width)
 
     stores[2].start()
-    for off in range(1, doms):
-        ask(off).wait_send()
-
-    @pl.loop(0, nblk)
-    def _(n):
-        for side in range(2):
-            near(side, n).wait_send()
-
-    @pl.loop(0, half)
-    def _(i):
-        for side in range(2):
-            far(side, i).wait_send()
-
-    for off in range(1, group):
-        give(off).wait_send()
-
-    for off in range(1, planes):
-        pass_on(off).wait_send()
+    wait_for(asked, ask_send)
+    wait_for(near_tab, near_send)
+    wait_for(far_tab, far_send)
+    wait_for(gath.at[pl.ds(0, group - 1)], gath_send)
+    wait_for(zsum.at[pl.ds(0, planes - 1)], zsum_send)
     for store in stores:
         store.wait()
 
@@ -494,21 +486,21 @@
             pltpu.VMEM((2, nblk // 2, ROWS, BLK), F32),
             pltpu.VMEM((2, nblk, ROWS, BLK), F32),
             pltpu.VMEM((2, nblk // 2, ROWS, BLK), F32),
-            pltpu.VMEM((3, BR, BLK), F32),
+            pltpu.VMEM((2, 3, BR, BLK), F32),
             pltpu.VMEM((32 * nblk, BLK), F32),
             pltpu.VMEM((group, 4, BLK), F32),
-            pltpu.VMEM((planes, BR + 8, BLK), F32),
+            pltpu.VMEM((planes, BR + 1, BLK), F32),
             pltpu.SemaphoreType.DMA((15,)),
+            pltpu.SemaphoreType.DMA,
             pltpu.SemaphoreType.DMA((doms - 1,)),
-            pltpu.SemaphoreType.DMA((doms - 1,)),
-            pltpu.SemaphoreType.DMA((2, nblk)),
-            pltpu.SemaphoreType.DMA((2, nblk)),
-            pltpu.SemaphoreType.DMA((2, nblk // 2)),
-            pltpu.SemaphoreType.DMA((2, nblk // 2)),
-            pltpu.SemaphoreType.DMA((group,)),
-            pltpu.SemaphoreType.DMA((group,)),
-            pltpu.SemaphoreType.DMA((planes,)),
-            pltpu.SemaphoreType.DMA((planes,)),
+            pltpu.SemaphoreType.DMA,
+            pltpu.SemaphoreType.DMA((nblk,)),
+            pltpu.SemaphoreType.DMA,
+            pltpu.SemaphoreType.DMA((nblk // 2,)),
+            pltpu.SemaphoreType.DMA,
+            pltpu.SemaphoreType.DMA,
+            pltpu.SemaphoreType.DMA,
+            pltpu.SemaphoreType.DMA,
             pltpu.SemaphoreType.REGULAR,
             pltpu.SemaphoreType.REGULAR,
             pltpu.SemaphoreType.REGULAR,

time: 39.6 us -> 37.8 us (0.955)
  Pallas kernels: 38.8 us -> 37 us
    pallas_call x1, Pallas kernels: 37.3 us -> 35.5 us  [on_device(): pl.pallas_call(functools.partial(step_kernel, sizes), out_shape=(jax.Shap...]
where the time goes in v4:
time: 37.8 us; the launch traced here: 37.6 us
  Pallas kernels  37 us (98%)
  between operations  0.64 us (2%)
    pallas_call x1, Pallas kernels, on_device(): pl.pallas_call(functools.partial(step_kernel, sizes), out_shape=(jax.Shap...  35.5 us
    pallas_call x1, Pallas kernels, on_device(): pl.pallas_call(store_kernel, out_shape=(jax.ShapeDtypeStruct((BR * nblk,...  1.52 us

profile of v4, /device:TPU:1, one launch (start us, length us, event | category | flops | bytes accessed | tf_op | source)
XLA Modules:
  0.0 37.6 jit_solution(15546939118691037171)
XLA Ops:
  0.6 35.5 %shard_map.130 = (f32[128,128]{1,0:T(8,128)}, f32[2,16,64]{2,1,0:T(8,128)}, f32[1997]{0:T(1024)}) custom-call(f32[7808,128]{1,0:T(8,128)} %bitcast.6, f32[7808,128]{1,0:T(8,128)} %bitcast.7, f32[61,64,61]{2,1,0:T(8,128)} %bitcast.8, f32[61,64,61]{2,1,0:T(8,128)} %bitcast.9, f32[64,61]{1,0:T(8,128)} %decay_hbm.1, f32[64,61]{1,0:T(8,128)} %weight_hbm.1, ...), custom_call_target="tpu_custom_call" | custom-call | tf_op jit(solution)/shard_map/pallas_call | solution.py:456
  36.1 1.5 %shard_map.131 = (f32[128,128]{1,0:T(8,128)}, f32[2,16,64]{2,1,0:T(8,128)}, f32[1997]{0:T(1024)}) custom-call(f32[128,128]{1,0:T(8,128)} %get-tuple-element.9.loglik, f32[2,16,64]{2,1,0:T(8,128)} %get-tuple-element.10.share, f32[1997]{0:T(1024)} %get-tuple-element.11.lengths), custom_call_target="tpu_custom_call" | custom-call | tf_op jit(solution)/shard_map/pallas_call | solution.py:524

commit v5 on v4

--- a/solution.py
+++ b/solution.py
@@ -48,9 +48,6 @@
     loglik_out,
     part_out,
     lengths_out,
-    loglik_v,
-    part_v,
-    new_v,
     top,
     bottom,
     top_s,
@@ -306,7 +303,7 @@
         first = like1 / like0
         second = like2 / like0 - first * first
         sites_w = pattern[pl.ds(n, 1), :].astype(F32)
-        loglik_v[pl.ds(n, BR, stride=nblk), :] = sites_w * jnp.log(like0)
+        loglik_out[pl.ds(n, BR, stride=nblk), :] = sites_w * jnp.log(like0)
         sums[pl.ds(n * 32, BR), :] = sites_w * first
         sums[pl.ds(n * 32 + BR, BR), :] = sites_w * second
 
@@ -317,12 +314,6 @@
         for side in range(2):
             one_block(side * half + i, side)
 
-    stores = [
-        pltpu.make_async_copy(loglik_v, loglik_out, local_sem.at[12]),
-        pltpu.make_async_copy(part_v, part_out, local_sem.at[13]),
-        pltpu.make_async_copy(new_v, lengths_out, local_sem.at[14]),
-    ]
-    stores[0].start()
     pl.semaphore_wait(line_sem, across - 1)
     pl.semaphore_wait(after_sem, 2)
 
@@ -397,9 +388,8 @@
 
     done = jnp.sum(zsum[...], axis=0)
     both = done[:BR]
-    part_v[0] = both[:, :owned]
-    part_v[1] = pltpu.roll(both, owned, 1)[:, :owned]
-    stores[1].start()
+    part_out[0] = both[:, :owned]
+    part_out[1] = pltpu.roll(both, owned, 1)[:, :owned]
     totals = jnp.broadcast_to(done[BR : BR + 1], (8, BLK))
     updated = times - totals / pltpu.roll(totals, BLK - BR, 1)
     tree = lengths_v.shape[0]
@@ -410,16 +400,13 @@
         new = lengths_v[pl.ds(start, width)].reshape(1, width)
         for b in range(BR):
             new = jnp.where(index[:, :width] + start == chosen[b], spots[b][:, :width], new)
-        new_v[pl.ds(start, width)] = new.reshape(width)
-
-    stores[2].start()
+        lengths_out[pl.ds(start, width)] = new.reshape(width)
+
     wait_for(asked, ask_send)
     wait_for(near_tab, near_send)
     wait_for(far_tab, far_send)
     wait_for(gath.at[pl.ds(0, group - 1)], gath_send)
     wait_for(zsum.at[pl.ds(0, planes - 1)], zsum_send)
-    for store in stores:
-        store.wait()
 
 
 def store_kernel(loglik, share, lengths, loglik_out, share_out, lengths_out, sem):
@@ -452,20 +439,18 @@
     flat = BR * STATES * nblk
     group = across * doms
     hbm = pl.BlockSpec(memory_space=pltpu.HBM)
+    vmem = pl.BlockSpec(memory_space=pltpu.VMEM)
     tree = branch_lengths.shape[0]
     loglik, share, lengths = pl.pallas_call(
         functools.partial(step_kernel, sizes),
         out_shape=(
-            jax.ShapeDtypeStruct((BR * nblk, BLK), F32),
-            jax.ShapeDtypeStruct((2, BR, owned), F32),
-            jax.ShapeDtypeStruct((tree,), F32),
-        ),
-        in_specs=[hbm] * 11,
-        out_specs=(hbm, hbm, hbm),
-        scratch_shapes=[
             pltpu.VMEM((BR * nblk, BLK), F32),
             pltpu.VMEM((2, BR, owned), F32),
             pltpu.VMEM((tree,), F32),
+        ),
+        in_specs=[hbm] * 11,
+        out_specs=(vmem, vmem, vmem),
+        scratch_shapes=[
             pltpu.VMEM((flat + (ROWS - STATES) * nblk, BLK), F32),
             pltpu.VMEM((flat + (ROWS - STATES) * nblk, BLK), F32),
             pltpu.VMEM((nblk, BR // 2, 2 * ROWS, 2 * BLK), BF16),
@@ -490,7 +475,7 @@
             pltpu.VMEM((32 * nblk, BLK), F32),
             pltpu.VMEM((group, 4, BLK), F32),
             pltpu.VMEM((planes, BR + 1, BLK), F32),
-            pltpu.SemaphoreType.DMA((15,)),
+            pltpu.SemaphoreType.DMA((12,)),
             pltpu.SemaphoreType.DMA,
             pltpu.SemaphoreType.DMA((doms - 1,)),
             pltpu.SemaphoreType.DMA,
@@ -528,9 +513,10 @@
             jax.ShapeDtypeStruct((2, BR, owned), F32),
             jax.ShapeDtypeStruct((tree,), F32),
         ),
-        in_specs=[pl.BlockSpec(memory_space=pltpu.VMEM)] * 3,
+        in_specs=[vmem] * 3,
         out_specs=(hbm, hbm, hbm),
         scratch_shapes=[pltpu.SemaphoreType.DMA((3,))],
+        compiler_params=pltpu.CompilerParams(vmem_limit_bytes=1024 * 1024),
     )(loglik, share, lengths)
     return (loglik.reshape(BR, 1, nblk * BLK), share, new_lengths)
 

time: 37.8 us -> 36.4 us (0.963)
  Pallas kernels: 37 us -> 35.6 us
    pallas_call x1, Pallas kernels: 1.52 us -> 0.66 us  [on_device(): pl.pallas_call(store_kernel, out_shape=(jax.ShapeDtypeStruct((BR * nblk,...]
    pallas_call x1, Pallas kernels: 35.5 us -> 35 us  [on_device(): pl.pallas_call(functools.partial(step_kernel, sizes), out_shape=(pltpu.VM...]
where the time goes in v5:
time: 36.4 us; the launch traced here: 36.3 us
  Pallas kernels  35.6 us (98%)
  between operations  0.64 us (2%)
    pallas_call x1, Pallas kernels, on_device(): pl.pallas_call(functools.partial(step_kernel, sizes), out_shape=(pltpu.VM...  35 us

profile of v5, /device:TPU:1, one launch (start us, length us, event | category | flops | bytes accessed | tf_op | source)
XLA Modules:
  0.0 36.3 jit_solution(12688445263871733289)
XLA Ops:
  0.6 35.0 %shard_map.130 = (f32[128,128]{1,0:T(8,128)S(1)}, f32[2,16,64]{2,1,0:T(8,128)S(1)}, f32[1997]{0:T(1024)S(1)}) custom-call(f32[7808,128]{1,0:T(8,128)} %bitcast.6, f32[7808,128]{1,0:T(8,128)} %bitcast.7, f32[61,64,61]{2,1,0:T(8,128)} %bitcast.8, f32[61,64,61]{2,1,0:T(8,128)} %bitcast.9, f32[64,61]{1,0:T(8,128)} %decay_hbm.1, f32[64,61]{1,0:T(8,128)} %weight_hbm.1, ...), custom_call_target="tpu_custom_call" | custom-call | tf_op jit(solution)/shard_map/pallas_call | solution.py:444
  35.6 0.7 %shard_map.131 = (f32[128,128]{1,0:T(8,128)}, f32[2,16,64]{2,1,0:T(8,128)}, f32[1997]{0:T(1024)}) custom-call(f32[128,128]{1,0:T(8,128)S(1)} %get-tuple-element.9.loglik, f32[2,16,64]{2,1,0:T(8,128)S(1)} %get-tuple-element.10.share, f32[1997]{0:T(1024)S(1)} %get-tuple-element.11.lengths), custom_call_target="tpu_custom_call" | custom-call | tf_op jit(solution)/shard_map/pallas_call | solution.py:509

commit v6 on v5

--- a/solution.py
+++ b/solution.py
@@ -71,6 +71,8 @@
     likes,
     sums,
     gath,
+    numbers,
+    hot,
     zsum,
     local_sem,
     ask_send,
@@ -81,6 +83,8 @@
     far_recv,
     gath_send,
     gath_recv,
+    num_send,
+    num_recv,
     zsum_send,
     zsum_recv,
     line_sem,
@@ -155,8 +159,8 @@
     tail = (ROWS - STATES, pitch, STATES)
     left[pl.ds(STATES, ROWS - STATES)] = jnp.zeros(tail, F32)
     right[pl.ds(STATES, ROWS - STATES)] = jnp.zeros(tail, F32)
-    left_rows = left.reshape(ROWS * pitch, STATES)
-    right_rows = right.reshape(ROWS * pitch, STATES)
+    left_rows = left.reshape((ROWS + 1) * pitch, STATES)
+    right_rows = right.reshape((ROWS + 1) * pitch, STATES)
     tail = (ROWS - STATES) * nblk
     top[pl.ds(BR * STATES * nblk, tail), :] = jnp.zeros((tail, BLK), F32)
     bottom[pl.ds(BR * STATES * nblk, tail), :] = jnp.zeros((tail, BLK), F32)
@@ -234,11 +238,10 @@
 
     for load in loads[:4] + small[1:]:
         load.wait()
-    loads[4].wait()
-    loads[5].wait()
-    split(top, top_s)
-    for off in range(1, doms):
-        ask(off).wait_recv()
+    ask(1).wait_recv()
+    ask(doms - 1).wait_recv()
+    direct(0, 1)
+    ask(2).wait_recv()
 
     @pl.loop(0, half)
     def _(i):
@@ -247,23 +250,51 @@
         for side in range(2):
             far(side, i).start()
 
-    direct(0, half - 2)
+    direct(1, half - 2)
 
     @pl.loop(0, nblk)
     def _(n):
         own_tab[n] = entry(blocks[0, n])
 
-    loads[6].wait()
+    for load in loads[4:]:
+        load.wait()
+    split(top, top_s)
     split(bottom, bottom_s)
     passed_on(0, 1)
     direct(half - 2, half - 1)
-    passed_on(1, 2)
+    passed_on(1, half - 1)
     direct(half - 1, half)
-    passed_on(2, half)
+    passed_on(half - 1, half)
 
     pl.semaphore_wait(next_sem, 2)
     for off in (2, planes - 2):
         pl.semaphore_signal(after_sem, inc=1, device_id=here(plane_at[off]), device_id_type=MESH)
+
+    def give(src, dst, sems, off):
+        return pltpu.make_async_remote_copy(
+            src_ref=src.at[rank],
+            dst_ref=dst.at[rank],
+            send_sem=sems[0],
+            recv_sem=sems[1],
+            device_id=group_peer(off),
+            device_id_type=MESH,
+        )
+
+    hops = lambda off, count: min(off, count - off)
+    spread_out = sorted(
+        range(1, group),
+        key=lambda off: -hops(off // doms // 2, across // 2) - hops(off % doms, doms),
+    )
+
+    pl.semaphore_wait(line_sem, across - 1)
+    lane_blk = lax.broadcasted_iota(jnp.int32, (1, BLK), 1) // 32
+    for g in range(2):
+        ids = jnp.zeros((1, BLK), F32)
+        for k in range(4):
+            ids = jnp.where(lane_blk == k, blocks[0, g * 4 + k].astype(F32), ids)
+        numbers[rank, pl.ds(g, 1), :] = ids
+    for off in spread_out:
+        give(numbers, numbers, (num_send, num_recv), off).start()
 
     lane1 = lax.broadcasted_iota(jnp.int32, (1, BLK), 1)
     times = jnp.zeros((1, BLK), F32)
@@ -271,7 +302,7 @@
         times = jnp.where(lane1 == b, lengths[chosen[b]], times)
     lane64 = lax.broadcasted_iota(jnp.int32, (ROWS, ROWS), 1)
 
-    def one_block(n, slot):
+    def prepared(n):
         got = own_tab[n]
         for side in range(2):
             got = got + recv_tab[side, n]
@@ -285,20 +316,21 @@
         lhs_r = jnp.concatenate([rv_hi, rv_hi, rv_lo], axis=1)
         expo_b = jnp.broadcast_to(exponent, (ROWS, BLK))
         decays = jnp.exp(exponent * times)
-
-        def stacked(ref, pair):
-            x = ref[n, pair]
-            return jnp.concatenate([x, x[:ROWS]], axis=0)
-
-        for b in range(0, BR, 2):
-            x, y = stacked(top_s, b // 2), stacked(bottom_s, b // 2)
-            joint = dot(lhs_l, x, ((1,), (0,))) * dot(lhs_r, y, ((1,), (0,)))
-            for c in range(2):
-                decayed = joint[:, c * BLK : (c + 1) * BLK] * decays[:, b + c : b + c + 1]
-                for power in range(3):
-                    likes[slot, power, pl.ds(b + c, 1), :] = jnp.sum(decayed, axis=0, keepdims=True)
-                    if power < 2:
-                        decayed = decayed * expo_b
+        return lhs_l, lhs_r, expo_b, decays
+
+    def two_branches(n, slot, b, lhs_l, lhs_r, expo_b, decays):
+        x, y = top_s[n, b // 2], bottom_s[n, b // 2]
+        x = jnp.concatenate([x, x[:ROWS]], axis=0)
+        y = jnp.concatenate([y, y[:ROWS]], axis=0)
+        joint = dot(lhs_l, x, ((1,), (0,))) * dot(lhs_r, y, ((1,), (0,)))
+        for c in range(2):
+            decayed = joint[:, c * BLK : (c + 1) * BLK] * decays[:, b + c : b + c + 1]
+            for power in range(3):
+                likes[slot, power, pl.ds(b + c, 1), :] = jnp.sum(decayed, axis=0, keepdims=True)
+                if power < 2:
+                    decayed = decayed * expo_b
+
+    def finished(n, slot):
         like0, like1, like2 = (likes[slot, power] for power in range(3))
         first = like1 / like0
         second = like2 / like0 - first * first
@@ -311,53 +343,37 @@
     def _(i):
         for side in range(2):
             wait_for(recv_tab.at[:, side * half + i], near_recv.at[side * half + i])
+        tables = [prepared(side * half + i) for side in range(2)]
+        for b in range(0, BR, 2):
+            for side in range(2):
+                two_branches(side * half + i, side, b, *tables[side])
         for side in range(2):
-            one_block(side * half + i, side)
-
-    pl.semaphore_wait(line_sem, across - 1)
+            finished(side * half + i, side)
+
     pl.semaphore_wait(after_sem, 2)
 
     ones = jnp.ones((8, BLK), BF16)
     total = sum(dot(ones, piece, ((1,), (1,))) for piece in three(sums[...]))
-    lane_blk = lax.broadcasted_iota(jnp.int32, (1, BLK), 1) // 32
     for g in range(2):
         gath[rank, pl.ds(g, 1), :] = total[0:1, g * BLK : (g + 1) * BLK]
-        ids = jnp.zeros((1, BLK), F32)
-        for k in range(4):
-            ids = jnp.where(lane_blk == k, blocks[0, g * 4 + k].astype(F32), ids)
-        gath[rank, pl.ds(2 + g, 1), :] = ids
-
-    def give(off):
-        return pltpu.make_async_remote_copy(
-            src_ref=gath.at[rank],
-            dst_ref=gath.at[rank],
-            send_sem=gath_send,
-            recv_sem=gath_recv,
-            device_id=group_peer(off),
-            device_id_type=MESH,
-        )
-
-    hops = lambda off, count: min(off, count - off)
-    spread_out = sorted(
-        range(1, group),
-        key=lambda off: -hops(off // doms // 2, across // 2) - hops(off % doms, doms),
-    )
     for off in spread_out:
-        give(off).start()
-
-    wait_for(gath.at[pl.ds(0, group - 1)], gath_recv)
-
-    vals = jnp.concatenate([gath[:, 0, :], gath[:, 1, :]], axis=0)
-    ids = jnp.concatenate([gath[:, 2, :], gath[:, 3, :]], axis=0)
+        give(gath, gath, (gath_send, gath_recv), off).start()
+
+    wait_for(numbers.at[pl.ds(0, group - 1)], num_recv)
+    ids = jnp.concatenate([numbers[:, 0, :], numbers[:, 1, :]], axis=0)
     local = lax.broadcasted_iota(jnp.int32, (2 * group, BLK), 1)
     mine = jnp.where(local < owned, local + me * owned, -1).astype(F32)
-    hot = jnp.concatenate(
-        [(ids[:, k * 32 : k * 32 + 1] == mine).astype(F32).astype(BF16) for k in range(4)], axis=1
-    )
+    for k in range(4):
+        one = (ids[:, k * 32 : k * 32 + 1] == mine).astype(F32).astype(BF16)
+        for copy in range(3):
+            hot[pl.ds(copy * 2 * group, 2 * group), pl.ds(k * BLK, BLK)] = one
+
+    wait_for(gath.at[pl.ds(0, group - 1)], gath_recv)
+    vals = jnp.concatenate([gath[:, 0, :], gath[:, 1, :]], axis=0)
     vals_t = jnp.transpose(vals)
     spread = dot(
         jnp.concatenate(three(vals_t), axis=1),
-        jnp.concatenate([hot, hot, hot], axis=0),
+        hot[...],
         ((1,), (0,)),
     )
     by_part = sum(spread[k * 32 : (k + 1) * 32, k * BLK : (k + 1) * BLK] for k in range(4))
@@ -406,6 +422,7 @@
     wait_for(near_tab, near_send)
     wait_for(far_tab, far_send)
     wait_for(gath.at[pl.ds(0, group - 1)], gath_send)
+    wait_for(numbers.at[pl.ds(0, group - 1)], num_send)
     wait_for(zsum.at[pl.ds(0, planes - 1)], zsum_send)
 
 
@@ -451,13 +468,13 @@
         in_specs=[hbm] * 11,
         out_specs=(vmem, vmem, vmem),
         scratch_shapes=[
-            pltpu.VMEM((flat + (ROWS - STATES) * nblk, BLK), F32),
-            pltpu.VMEM((flat + (ROWS - STATES) * nblk, BLK), F32),
+            pltpu.VMEM((flat + (ROWS - STATES + 1) * nblk, BLK), F32),
+            pltpu.VMEM((flat + (ROWS - STATES + 1) * nblk, BLK), F32),
             pltpu.VMEM((nblk, BR // 2, 2 * ROWS, 2 * BLK), BF16),
             pltpu.VMEM((nblk, BR // 2, 2 * ROWS, 2 * BLK), BF16),
             pltpu.VMEM((nblk, ROWS, BLK), F32),
-            pltpu.VMEM((ROWS, owned + 8, STATES), F32),
-            pltpu.VMEM((ROWS, owned + 8, STATES), F32),
+            pltpu.VMEM((ROWS + 1, owned + 8, STATES), F32),
+            pltpu.VMEM((ROWS + 1, owned + 8, STATES), F32),
             pltpu.VMEM((owned, STATES), F32),
             pltpu.VMEM((owned, STATES), F32),
             pltpu.VMEM((nblk, BLK), jnp.int32),
@@ -473,7 +490,9 @@
             pltpu.VMEM((2, nblk // 2, ROWS, BLK), F32),
             pltpu.VMEM((2, 3, BR, BLK), F32),
             pltpu.VMEM((32 * nblk, BLK), F32),
-            pltpu.VMEM((group, 4, BLK), F32),
+            pltpu.VMEM((group, 2, BLK), F32),
+            pltpu.VMEM((group, 2, BLK), F32),
+            pltpu.VMEM((6 * group, 4 * BLK), BF16),
             pltpu.VMEM((planes, BR + 1, BLK), F32),
             pltpu.SemaphoreType.DMA((12,)),
             pltpu.SemaphoreType.DMA,
@@ -482,6 +501,8 @@
             pltpu.SemaphoreType.DMA((nblk,)),
             pltpu.SemaphoreType.DMA,
             pltpu.SemaphoreType.DMA((nblk // 2,)),
+            pltpu.SemaphoreType.DMA,
+            pltpu.SemaphoreType.DMA,
             pltpu.SemaphoreType.DMA,
             pltpu.SemaphoreType.DMA,
             pltpu.SemaphoreType.DMA,

time: 36.4 us -> 35.6 us (0.978)
  Pallas kernels: 35.6 us -> 34.9 us
    pallas_call x1, Pallas kernels: 35 us -> 34.2 us  [on_device(): pl.pallas_call(functools.partial(step_kernel, sizes), out_shape=(pltpu.VM...]
where the time goes in v6:
time: 35.6 us; the launch traced here: 35.5 us
  Pallas kernels  34.9 us (98%)
  between operations  0.64 us (2%)
    pallas_call x1, Pallas kernels, on_device(): pl.pallas_call(functools.partial(step_kernel, sizes), out_shape=(pltpu.VM...  34.2 us

profile of v6, /device:TPU:1, one launch (start us, length us, event | category | flops | bytes accessed | tf_op | source)
XLA Modules:
  0.0 35.5 jit_solution(3448494158112293808)
XLA Ops:
  0.6 34.2 %shard_map.130 = (f32[128,128]{1,0:T(8,128)S(1)}, f32[2,16,64]{2,1,0:T(8,128)S(1)}, f32[1997]{0:T(1024)S(1)}) custom-call(f32[7808,128]{1,0:T(8,128)} %bitcast.6, f32[7808,128]{1,0:T(8,128)} %bitcast.7, f32[61,64,61]{2,1,0:T(8,128)} %bitcast.8, f32[61,64,61]{2,1,0:T(8,128)} %bitcast.9, f32[64,61]{1,0:T(8,128)} %decay_hbm.1, f32[64,61]{1,0:T(8,128)} %weight_hbm.1, ...), custom_call_target="tpu_custom_call" | custom-call | tf_op jit(solution)/shard_map/pallas_call | solution.py:461
  34.9 0.7 %shard_map.131 = (f32[128,128]{1,0:T(8,128)}, f32[2,16,64]{2,1,0:T(8,128)}, f32[1997]{0:T(1024)}) custom-call(f32[128,128]{1,0:T(8,128)S(1)} %get-tuple-element.9.loglik, f32[2,16,64]{2,1,0:T(8,128)S(1)} %get-tuple-element.10.share, f32[1997]{0:T(1024)S(1)} %get-tuple-element.11.lengths), custom_call_target="tpu_custom_call" | custom-call | tf_op jit(solution)/shard_map/pallas_call | solution.py:530

commit v7 on v6

--- a/solution.py
+++ b/solution.py
@@ -238,9 +238,11 @@
 
     for load in loads[:4] + small[1:]:
         load.wait()
-    ask(1).wait_recv()
-    ask(doms - 1).wait_recv()
-    direct(0, 1)
+    for side, off in ((0, 1), (1, doms - 1)):
+        ask(off).wait_recv()
+        n = (1 - side) * half
+        near_tab[side, n] = entry(asked[near_ids[side], 0, n])
+        near(side, n).start()
     ask(2).wait_recv()
 
     @pl.loop(0, half)

time: 35.6 us -> 35.5 us (level)
  no operation moved by 1% of the time
where the time goes in v7:
time: 35.5 us; the launch traced here: 35.4 us
  Pallas kernels  34.8 us (98%)
  between operations  0.64 us (2%)
    pallas_call x1, Pallas kernels, on_device(): pl.pallas_call(functools.partial(step_kernel, sizes), out_shape=(pltpu.VM...  34.1 us

profile of v7, /device:TPU:1, one launch (start us, length us, event | category | flops | bytes accessed | tf_op | source)
XLA Modules:
  0.0 35.4 jit_solution(12359077748684510961)
XLA Ops:
  0.6 34.1 %shard_map.130 = (f32[128,128]{1,0:T(8,128)S(1)}, f32[2,16,64]{2,1,0:T(8,128)S(1)}, f32[1997]{0:T(1024)S(1)}) custom-call(f32[7808,128]{1,0:T(8,128)} %bitcast.6, f32[7808,128]{1,0:T(8,128)} %bitcast.7, f32[61,64,61]{2,1,0:T(8,128)} %bitcast.8, f32[61,64,61]{2,1,0:T(8,128)} %bitcast.9, f32[64,61]{1,0:T(8,128)} %decay_hbm.1, f32[64,61]{1,0:T(8,128)} %weight_hbm.1, ...), custom_call_target="tpu_custom_call" | custom-call | tf_op jit(solution)/shard_map/pallas_call | solution.py:463
  34.8 0.7 %shard_map.131 = (f32[128,128]{1,0:T(8,128)}, f32[2,16,64]{2,1,0:T(8,128)}, f32[1997]{0:T(1024)}) custom-call(f32[128,128]{1,0:T(8,128)S(1)} %get-tuple-element.9.loglik, f32[2,16,64]{2,1,0:T(8,128)S(1)} %get-tuple-element.10.share, f32[1997]{0:T(1024)S(1)} %get-tuple-element.11.lengths), custom_call_target="tpu_custom_call" | custom-call | tf_op jit(solution)/shard_map/pallas_call | solution.py:532
